TPU v7x, 128 devices: a whole 4x4x4 slice. The times are simulated.
128 devices in a mesh: data: 128 (over z, y, x, core).
Axes of the slice: x: 4, y: 4, z: 4, core: 2. Of those that a mesh axis runs over, the one named last changes fastest.
Arguments:
- x_tokens: bfloat16 [262144, 768], P('data')
- dh_out: bfloat16 [262144, 768], P('data')
- w_up: bfloat16 [2, 768, 2048], replicated
- w_down: bfloat16 [2, 2048, 768], replicated
- proj_up: bfloat16 [2, 768, 256], replicated
- proj_down: bfloat16 [2, 768, 256], replicated
- mom_up: float32 [2, 256, 2048], P(None, None, 'data')
- var_up: float32 [2, 256, 2048], P(None, None, 'data')
- mom_down: float32 [2, 2048, 256], P(None, 'data')
- var_down: float32 [2, 2048, 256], P(None, 'data')
Outputs:
- output 1: bfloat16 [2, 768, 2048], replicated
- output 2: bfloat16 [2, 2048, 768], replicated
- output 3: float32 [2, 256, 2048], P(None, None, 'data')
- output 4: float32 [2, 256, 2048], P(None, None, 'data')
- output 5: float32 [2, 2048, 256], P(None, 'data')
- output 6: float32 [2, 2048, 256], P(None, 'data')
All inputs are finite; a program needn't handle non-finite values.
Results may differ from a plain program's by a relative error of at most 0.0072576.
Values are sent between devices in bfloat16 or wider.
A program may use at most 1 GiB of HBM per device.

v0:
```python
import jax
import jax.numpy as jnp
from jax import lax
from jax.sharding import PartitionSpec as P

BETA_ONE = 0.9
BETA_TWO = 0.999
EPSILON = 1e-8
STEP = 4
LEARN_RATE = 0.02
ALPHA_SCALE = 0.25


def contract_rows(lhs, rhs):
    return lax.dot_general(lhs, rhs, (((0,), (0,)), ((), ())), preferred_element_type=jnp.float32)


def contract_cols(lhs, rhs):
    return lax.dot_general(lhs, rhs, (((1,), (1,)), ((), ())), preferred_element_type=jnp.float32)


def projected_grads(x_rows, dh_rows, w_up, w_down, proj_up, proj_down):
    layers = w_up.shape[0]
    hidden = [x_rows]
    act_list = []
    pull_list = []
    for layer_idx in range(layers):
        pre_act = jnp.dot(hidden[layer_idx], w_up[layer_idx], preferred_element_type=jnp.float32)
        gelu_val, gelu_pull = jax.vjp(jax.nn.gelu, pre_act)
        act_val = gelu_val.astype(jnp.bfloat16)
        down_out = jnp.dot(act_val, w_down[layer_idx], preferred_element_type=jnp.float32)
        hidden.append((hidden[layer_idx] + down_out).astype(jnp.bfloat16))
        act_list.append(act_val)
        pull_list.append(gelu_pull)
    grad_rows = dh_rows
    up_parts = [None] * layers
    down_parts = [None] * layers
    for layer_idx in reversed(range(layers)):
        v_proj = jnp.dot(grad_rows, proj_down[layer_idx], preferred_element_type=jnp.float32).astype(jnp.bfloat16)
        down_parts[layer_idx] = contract_rows(act_list[layer_idx], v_proj)
        d_act = contract_cols(grad_rows, w_down[layer_idx])
        d_pre = pull_list[layer_idx](d_act)[0].astype(jnp.bfloat16)
        u_proj = jnp.dot(hidden[layer_idx], proj_up[layer_idx], preferred_element_type=jnp.float32).astype(jnp.bfloat16)
        up_parts[layer_idx] = contract_rows(u_proj, d_pre)
        if layer_idx > 0:
            grad_rows = (grad_rows + contract_cols(d_pre, w_up[layer_idx])).astype(jnp.bfloat16)
    return jnp.stack(up_parts), jnp.stack(down_parts)


def adam_shard(moment, variance, grad_red):
    new_mom = BETA_ONE * moment + (1.0 - BETA_ONE) * grad_red
    new_var = BETA_TWO * variance + (1.0 - BETA_TWO) * grad_red * grad_red
    bias_one = 1.0 - BETA_ONE ** STEP
    bias_two = 1.0 - BETA_TWO ** STEP
    direction = (new_mom / bias_one) / (jnp.sqrt(new_var / bias_two) + EPSILON)
    return new_mom, new_var, direction.astype(jnp.bfloat16)


def solution(mesh):
    def local_step(x_loc, dh_loc, w_up, w_down, proj_up, proj_down, mom_up, var_up, mom_down, var_down):
        micro = x_loc.shape[0] // 2
        scattered = []
        for micro_idx in range(2):
            x_micro = x_loc[micro_idx * micro:(micro_idx + 1) * micro]
            dh_micro = dh_loc[micro_idx * micro:(micro_idx + 1) * micro]
            part_up, part_down = projected_grads(x_micro, dh_micro, w_up, w_down, proj_up, proj_down)
            sum_up = lax.psum_scatter(part_up, 'data', scatter_dimension=2, tiled=True)
            sum_down = lax.psum_scatter(part_down, 'data', scatter_dimension=1, tiled=True)
            scattered.append((sum_up, sum_down))
        red_up = scattered[0][0] + scattered[1][0]
        red_down = scattered[0][1] + scattered[1][1]
        new_mom_up, new_var_up, dir_up = adam_shard(mom_up, var_up, red_up)
        new_mom_down, new_var_down, dir_down = adam_shard(mom_down, var_down, red_down)
        shard_cols = mom_up.shape[2]
        col_start = lax.axis_index('data') * shard_cols
        w_up_loc = lax.dynamic_slice_in_dim(w_up, col_start, shard_cols, axis=2)
        w_down_loc = lax.dynamic_slice_in_dim(w_down, col_start, shard_cols, axis=1)
        delta_up = jnp.einsum('ldr,lrf->ldf', proj_up, dir_up, preferred_element_type=jnp.float32)
        delta_down = jnp.einsum('lfr,ldr->lfd', dir_down, proj_down, preferred_element_type=jnp.float32)
        new_up_loc = (w_up_loc - (LEARN_RATE * ALPHA_SCALE) * delta_up).astype(jnp.bfloat16)
        new_down_loc = (w_down_loc - (LEARN_RATE * ALPHA_SCALE) * delta_down).astype(jnp.bfloat16)
        new_w_up = lax.all_gather(new_up_loc, 'data', axis=2, tiled=True)
        new_w_down = lax.all_gather(new_down_loc, 'data', axis=1, tiled=True)
        return new_w_up, new_w_down, new_mom_up, new_var_up, new_mom_down, new_var_down

    tok_spec = P('data', None)
    up_spec = P(None, None, 'data')
    down_spec = P(None, 'data', None)
    return jax.shard_map(
        local_step,
        mesh=mesh,
        in_specs=(tok_spec, tok_spec, P(), P(), P(), P(), up_spec, up_spec, down_spec, down_spec),
        out_specs=(P(), P(), up_spec, up_spec, down_spec, down_spec),
        check_vma=False,
    )
```

profile of v0, /device:TPU:1, one launch (start us, length us, event | category | flops | bytes accessed | tf_op | source)
XLA Modules:
  0.0 1104.6 jit_solution(261310183233518124)
XLA Ops:
  7.2 0.0 all-reduce.3.cloned.1.call-start
  7.2 3.0 convolution_convert_fusion.5
  10.2 2.0 convolution_convert_fusion.7
  12.3 0.0 slice-start.2
  12.3 7.3 fusion.60
  19.6 3.4 fusion.58
  23.1 5.0 add_convert_fusion.1
  28.1 5.7 fusion.36
  33.9 11.3 %fusion.27 = bf16[1024,2048]{1,0:T(8,128)(2,1)} fusion(f32[1024,2048]{1,0:T(8,128)} %fusion.36, bf16[2,2048,768]{2,1,0:T(8,128)(2,1)S(1)} %bitcast.119, bf16[2048,768]{1,0:T(8,128)(2,1)S(1)} %copy-done.13), kind=kOutput, calls=%fused_computation.35 | convolution fusion | flops 3263168512 | bytes 17301504 | tf_op jit(solution)/shard_map/dot_general | solution.py:19
  45.2 5.1 convolution_bitcast_fusion.2
  50.4 0.0 slice-start
  50.4 0.0 slice-start.4
  50.4 8.3 add_convert_fusion
  58.7 9.4 add_convert_fusion.3
  68.1 3.4 fusion.40
  71.6 3.2 copy-done.19
  74.8 20.0 %fusion.13 = bf16[1024,2048]{1,0:T(8,128)(2,1)} fusion(f32[1024,2048]{1,0:T(8,128)S(1)} %fusion.40, bf16[2,2048,768]{2,1,0:T(8,128)(2,1)S(1)} %bitcast.121, bf16[2048,768]{1,0:T(8,128)(2,1)S(1)} %copy-done.14), kind=kOutput, calls=%fused_computation.21 | convolution fusion | flops 3263168512 | bytes 17301504 | tf_op jit(solution)/shard_map/dot_general | solution.py:19
  94.8 6.5 convolution_bitcast_fusion.3
  101.3 8.2 add_convert_fusion.2
  109.5 12.0 %fusion.79 = f32[1,256,2048]{2,1,0:T(8,128)} fusion(bf16[1024,256]{1,0:T(8,128)(2,1)S(1)} %copy-done.17, f32[1024,2048]{1,0:T(8,128)} %copy-done.18, bf16[1024,768]{1,0:T(8,128)(2,1)} %add_convert_fusion, bf16[2,2048,768]{2,1,0:T(8,128)(2,1)} %param.13), kind=kOutput, calls=%fused_computation.79 | convolution fusion | flops 4336910336 | bytes 15728640 | tf_op jit(solution)/shard_map/dot_general | solution.py:15
  121.5 12.1 %fusion.74 = f32[1,256,2048]{2,1,0:T(8,128)} fusion(bf16[1024,256]{1,0:T(8,128)(2,1)S(1)} %convolution_convert_fusion.7, f32[1024,2048]{1,0:T(8,128)} %fusion.60, bf16[1024,768]{1,0:T(8,128)(2,1)} %add_convert_fusion.2, bf16[2,2048,768]{2,1,0:T(8,128)(2,1)} %param.13), kind=kOutput, calls=%fused_computation.78 | convolution fusion | flops 4336910336 | bytes 15728640 | tf_op jit(solution)/shard_map/dot_general | solution.py:15
  133.6 5.8 maximum_add_fusion
  139.3 7.3 copy.34
  146.6 0.0 all-reduce.3.cloned.1.call-update
  146.7 0.3 reduce-scatter.2.cloned.1.call-start
  146.9 7.6 fusion.84
  154.5 9.0 convolution_bitcast_fusion
  163.5 9.0 convolution_bitcast_fusion.1
  172.5 9.2 fusion.85
  181.6 5.4 maximum_add_fusion.1
  187.1 0.0 reduce-scatter.2.cloned.1.call-update
  187.1 0.0 all-gather.3.cloned.1.call-start
  187.1 1.2 constant_dynamic-slice_fusion.1
  188.3 0.1 copy.39
  188.5 116.8 %all-reduce.3.cloned.1.call-done = f32[2,256,2048]{1,0,2:T(2,128)} async-done(((f32[2,256,2048]{1,0,2:T(2,128)}), f32[2,256,2048]{1,0,2:T(2,128)}) %all-reduce.3.cloned.1.call-update) | async-done | bytes 4194320
  305.3 0.8 constant_dynamic-slice_fusion
  306.1 0.0 copy-start.4
  306.1 2.1 fusion.117
  308.2 0.0 all-gather.3.cloned.1.call-update
  308.2 0.0 all-gather.5.cloned.1.call-start
  308.3 641.9 %reduce-scatter.2.cloned.1.call-done = f32[2,16,256]{2,1,0:T(8,128)} async-done(((f32[2,2048,256]{2,1,0:T(8,128)}), f32[2,16,256]{2,1,0:T(8,128)}) %reduce-scatter.2.cloned.1.call-update) | async-done | bytes 32784 | tf_op jit(solution)/shard_map/reduce_scatter | solution.py:68
  950.2 0.8 multiply_add_fusion
  951.0 1.8 fusion.118
  952.7 0.0 all-gather.5.cloned.1.call-update
  952.7 70.0 %all-gather.3.cloned.1.call-done = bf16[2,768,2048]{1,2,0:T(8,128)(2,1)} async-done(((bf16[2,768,16]{1,2,0:T(8,128)(2,1)}), bf16[2,768,2048]{1,2,0:T(8,128)(2,1)}) %all-gather.3.cloned.1.call-update) | async-done | bytes 6291472 | tf_op jit(solution)/shard_map/all_gather | solution.py:82
  1022.7 8.6 copy.38
  1031.3 60.4 %all-gather.5.cloned.1.call-done = bf16[2,2048,768]{2,1,0:T(8,128)(2,1)} async-done(((bf16[2,16,768]{2,1,0:T(8,128)(2,1)}), bf16[2,2048,768]{2,1,0:T(8,128)(2,1)}) %all-gather.5.cloned.1.call-update) | async-done | bytes 6291472 | tf_op jit(solution)/shard_map/all_gather | solution.py:83
  1091.7 5.9 copy.44
  (51 shorter events, 0.1 us)
Async XLA Ops:
  7.2 298.1 %all-reduce.3.cloned.1.call-start = ((), (), s32[]{:S(2)}) async-start(), calls=%async_computation.4 | async-start | bytes 8388608
  7.2 5.1 copy-start.10
  12.3 7.3 copy-start.11
  12.3 10.7 slice-start.2
  19.6 3.4 slice-start.3
  23.1 5.0 copy-start.18
  28.1 5.7 copy-start.15
  28.1 5.7 copy-start.13
  33.9 11.3 %copy-start.1 = (bf16[2,768,256]{2,1,0:T(8,128)(2,1)S(1)}, bf16[2,768,256]{2,1,0:T(8,128)(2,1)}, u32[]{:S(2)}) copy-start(bf16[2,768,256]{2,1,0:T(8,128)(2,1)} %param.14) | copy-start | bytes 2359300
  50.3 8.3 copy-start.12
  50.4 17.7 %slice-start = ((s8[6291456]{0:T(1024)(128)(4,1)}), s8[4194304]{0:T(1024)(128)(4,1)S(1)}, s32[]{:S(2)}) async-start(s8[6291456]{0:T(1024)(128)(4,1)} %bitcast.116), calls=%async_computation.5 | async-start | bytes 8388608
  50.4 24.5 %slice-start.4 = ((s8[6291456]{0:T(1024)(128)(4,1)}), s8[4194304]{0:T(1024)(128)(4,1)S(1)}, s32[]{:S(2)}) async-start(s8[6291456]{0:T(1024)(128)(4,1)} %bitcast.120), calls=%async_computation.9 | async-start | bytes 8388608
  58.7 9.4 slice-start.1
  58.7 16.2 %slice-start.5 = ((s8[6291456]{0:T(1024)(128)(4,1)}), s8[2097152]{0:T(1024)(128)(4,1)S(1)}, s32[]{:S(2)}) async-start(s8[6291456]{0:T(1024)(128)(4,1)} %bitcast.120), calls=%async_computation.10 | async-start | bytes 4194304
  68.1 3.4 copy-start.16
  68.1 6.7 copy-start.14
  71.6 3.3 copy-start.19
  101.3 8.2 copy-start.17
  139.3 7.6 copy-start
  146.7 803.5 %reduce-scatter.2.cloned.1.call-start = ((), (), s32[]{:S(2)}) async-start(), calls=%async_computation.3 | async-start | bytes 4227072 | tf_op jit(solution)/shard_map/reduce_scatter | solution.py:68
  181.6 124.4 %copy-start.6 = (f32[2,256,16]{1,2,0:T(8,128)S(1)}, f32[2,256,16]{1,2,0:T(8,128)}, u32[]{:S(2)}) copy-start(f32[2,256,16]{1,2,0:T(8,128)} %param.16) | copy-start | bytes 98308
  181.6 124.4 %copy-start.7 = (f32[2,256,16]{1,2,0:T(8,128)S(1)}, f32[2,256,16]{1,2,0:T(8,128)}, u32[]{:S(2)}) copy-start(f32[2,256,16]{1,2,0:T(8,128)} %param.17) | copy-start | bytes 98308
  187.1 763.1 %copy-start.8 = (f32[2,16,256]{2,1,0:T(8,128)S(1)}, f32[2,16,256]{2,1,0:T(8,128)}, u32[]{:S(2)}) copy-start(f32[2,16,256]{2,1,0:T(8,128)} %param.18) | copy-start | bytes 98308
  187.1 763.1 %copy-start.9 = (f32[2,16,256]{2,1,0:T(8,128)S(1)}, f32[2,16,256]{2,1,0:T(8,128)}, u32[]{:S(2)}) copy-start(f32[2,16,256]{2,1,0:T(8,128)} %param.19) | copy-start | bytes 98308
  187.1 835.6 %all-gather.3.cloned.1.call-start = ((), (), s32[]{:S(2)}) async-start(), calls=%async_computation.1 | async-start | bytes 6340608 | tf_op jit(solution)/shard_map/all_gather | solution.py:82
  306.1 725.2 %copy-start.4 = (f32[2,256,16]{1,2,0:T(8,128)}, f32[2,256,16]{1,2,0:T(8,128)S(1)}, u32[]{:S(2)}) copy-start(f32[2,256,16]{1,2,0:T(8,128)S(1)} %get-tuple-element.36) | copy-start | bytes 98308
  306.1 725.2 %copy-start.5 = (f32[2,256,16]{1,2,0:T(8,128)}, f32[2,256,16]{1,2,0:T(8,128)S(1)}, u32[]{:S(2)}) copy-start(f32[2,256,16]{1,2,0:T(8,128)S(1)} %get-tuple-element.37) | copy-start | bytes 98308
  308.2 783.5 %all-gather.5.cloned.1.call-start = ((), (), s32[]{:S(2)}) async-start(), calls=%async_computation.2 | async-start | bytes 6340608 | tf_op jit(solution)/shard_map/all_gather | solution.py:83
  950.9 80.4 %copy-start.2 = (f32[2,16,256]{2,1,0:T(8,128)}, f32[2,16,256]{2,1,0:T(8,128)S(1)}, u32[]{:S(2)}) copy-start(f32[2,16,256]{2,1,0:T(8,128)S(1)} %get-tuple-element.38) | copy-start | bytes 98308
  950.9 80.4 %copy-start.3 = (f32[2,16,256]{2,1,0:T(8,128)}, f32[2,16,256]{2,1,0:T(8,128)S(1)}, u32[]{:S(2)}) copy-start(f32[2,16,256]{2,1,0:T(8,128)S(1)} %get-tuple-element.39) | copy-start | bytes 98308
Sparse Core Ops, SparseCore 0:
  146.8 158.4 all-reduce.2
  308.2 641.8 reduce-scatter.1
  953.6 69.0 all-gather.2
  1026.0 65.6 all-gather.4
where the time goes:
time: 1110 us; the launch traced here: 1100 us
  waiting for transfers between devices  889 us (80%)
  matrix products  161 us (15%)
  local copies, waits for them, and re-layouts  27.2 us (2%)
  between operations  14.5 us (1%)
  other arithmetic  12 us (1%)
    reduce_scatter x1, waiting for transfers between devices, local_step(): lax.psum_scatter(part_down, 'data', scatter_dimension=1, tiled=True)  642 us
    unnamed x5, waiting for transfers between devices  117 us
    dot_general x8, matrix products, contract_rows(): lax.dot_general(lhs, rhs, (((0,), (0,)), ((), ())), preferred_element_typ...  70.4 us
    all_gather x1, waiting for transfers between devices, local_step(): new_w_up = lax.all_gather(new_up_loc, 'data', axis=2, tiled=True)  70 us
    all_gather x1, waiting for transfers between devices, local_step(): new_w_down = lax.all_gather(new_down_loc, 'data', axis=1, tiled=True)  60.4 us
    dot_general x4, matrix products, contract_cols(): lax.dot_general(lhs, rhs, (((1,), (1,)), ((), ())), preferred_element_typ...  47.7 us
  transfers between devices with their start and end apart: 4, of which 4 were waited for; matrix products, arithmetic and copies ran while one was open for 5% of the time, Pallas kernels for 0%

commit v1 on v0

v1 whole, which is shorter than its diff:
```python
import jax
import jax.numpy as jnp
from jax import lax
from jax.experimental import pallas as pl
from jax.experimental.pallas import tpu as pltpu
from jax.sharding import PartitionSpec as P

BETA_ONE = 0.9
BETA_TWO = 0.999
EPSILON = 1e-8
STEP = 4
LEARN_RATE = 0.02
ALPHA_SCALE = 0.25
SCALE = LEARN_RATE * ALPHA_SCALE
GELU_A = 0.7978845608028654
GELU_B = 0.044715
MESH = pl.DeviceIdType.MESH
F32, BF16 = jnp.float32, jnp.bfloat16

BLOCK = 512
TILE = 256
BLOCKS = 4
TILES = 8

ORDERS = ((2, 1, 0), (1, 0, 2), (0, 2, 1))
COLOURS = ((0, 1, 2), (1, 2, 0), (2, 0, 1), (0, 1, 2))
PIECES = ((0, 0, 256), (1, 0, 128), (1, 128, 128))
UNITS = ((0, 1), (2, 0), (1, 2), (0, 1))


def dot(lhs, rhs):
    return jnp.dot(lhs, rhs, preferred_element_type=F32)


def dot_t(lhs, rhs):
    return lax.dot_general(lhs, rhs, (((1,), (1,)), ((), ())), preferred_element_type=F32)


def gelu_pair(z):
    sq = z * z
    cdf = 0.5 + 0.5 * jnp.tanh(z * (GELU_A + (GELU_A * GELU_B) * sq))
    act = z * cdf
    slope = cdf + act * ((1.0 - cdf) * (2.0 * GELU_A + (6.0 * GELU_A * GELU_B) * sq))
    return act, slope


def adam_shard(moment, variance, grad_red):
    new_mom = BETA_ONE * moment + (1.0 - BETA_ONE) * grad_red
    new_var = BETA_TWO * variance + (1.0 - BETA_TWO) * grad_red * grad_red
    bias_one = 1.0 - BETA_ONE ** STEP
    bias_two = 1.0 - BETA_TWO ** STEP
    direction = (new_mom / bias_one) / (jnp.sqrt(new_var / bias_two) + EPSILON)
    return new_mom, new_var, direction.astype(BF16)


def block_rows(i):
    return pl.ds(pl.multiple_of(i * BLOCK, BLOCK), BLOCK)


def tile_cols(n):
    return pl.ds(pl.multiple_of(n * TILE, TILE), TILE)


def grad_kernel(x_hbm, dh_hbm, wu_hbm, wd_hbm, pu_hbm, pd_hbm, r_out, gp_hbm,
                h, g, wu, wd, pu, pd, act, dz, ut0, ut1, vt, gp, tile, rtmp, in_sem, gp_sem, r_sem):
    loads = {}

    def load(name, src, dst):
        cp = pltpu.make_async_copy(src, dst, in_sem.at[len(loads)])
        cp.start()
        loads[name] = cp

    load("x", x_hbm, h)
    load("wu0", wu_hbm.at[0], wu.at[0])
    load("pu", pu_hbm, pu)
    load("wd0", wd_hbm.at[0], wd.at[0])
    load("dh", dh_hbm, g)
    load("pd", pd_hbm, pd)
    load("wu1", wu_hbm.at[1], wu.at[1])
    load("wd1", wd_hbm.at[1], wd.at[1])

    def slope_out(rb):
        return pltpu.make_async_copy(gp, gp_hbm.at[:, rb], gp_sem.at[0])

    def slope_in(n, half):
        return pltpu.make_async_copy(gp_hbm.at[n], gp.at[pl.ds(4 * half, 4)], gp_sem.at[half])

    def emit_copy(m, n, slot):
        return pltpu.make_async_copy(
            rtmp.at[slot], r_out.at[m, n // 2, pl.ds(2 * lax.rem(n, 2), 2)], r_sem.at[slot])

    def emit(m, n, slot, part):
        rtmp[slot] = part.T.reshape(2, 4, 2, 2, 8, 256)
        emit_copy(m, n, slot).start()

    for name in ("x", "wu0", "pu", "wd0"):
        loads[name].wait()

    def forward_zero(rb, _):
        rows = block_rows(rb)
        hidden = h[rows]
        ut0[:, rows] = dot(hidden, pu[0]).astype(BF16).T
        for n in range(TILES):
            cols = slice(TILE * n, TILE * n + TILE)
            value, slope = gelu_pair(dot(hidden, wu[0, :, cols]))
            act[rows, cols] = value.astype(BF16)
            gp[n] = slope
        cp = slope_out(rb)
        cp.start()
        h[rows] = (hidden + dot(act[rows], wd[0])).astype(BF16)
        cp.wait()
        return 0

    lax.fori_loop(0, BLOCKS, forward_zero, 0)
    for name in ("dh", "pd", "wu1", "wd1"):
        loads[name].wait()

    def project_one(rb, _):
        rows = block_rows(rb)
        ut1[:, rows] = dot(h[rows], pu[1]).astype(BF16).T
        vt[:, rows] = dot(g[rows], pd[1]).astype(BF16).T
        return 0

    lax.fori_loop(0, BLOCKS, project_one, 0)

    def layer_one(n, _):
        cols = tile_cols(n)
        slot = 2 * lax.rem(n, 2)

        @pl.when(n >= 2)
        def _():
            emit_copy(3, n - 2, slot).wait()
            emit_copy(2, n - 2, slot + 1).wait()

        for rc in range(BLOCKS):
            rows = slice(BLOCK * rc, BLOCK * rc + BLOCK)
            value, slope = gelu_pair(dot(h[rows], wu[1, :, cols]))
            tile[rows] = value.astype(BF16)
            dz[rows, cols] = (slope * dot_t(g[rows], wd[1, cols, :])).astype(BF16)
        emit(3, n, slot, dot(vt[...], tile[...]))
        emit(2, n, slot + 1, dot(ut1[...], dz[:, cols]))
        return 0

    lax.fori_loop(0, TILES, layer_one, 0)
    slope_in(0, 0).start()

    def input_grad(rb, _):
        rows = block_rows(rb)
        grad = (g[rows] + dot_t(dz[rows], wu[1])).astype(BF16)
        g[rows] = grad
        vt[:, rows] = dot(grad, pd[0]).astype(BF16).T
        return 0

    lax.fori_loop(0, BLOCKS, input_grad, 0)
    for n in (TILES - 2, TILES - 1):
        emit_copy(3, n, 2 * (n % 2)).wait()
        emit_copy(2, n, 2 * (n % 2) + 1).wait()

    def down_zero(n, _):
        slot = lax.rem(n, 2)

        @pl.when(n >= 2)
        def _():
            emit_copy(1, n - 2, slot).wait()

        emit(1, n, slot, dot(vt[...], act[:, tile_cols(n)]))
        return 0

    lax.fori_loop(0, TILES, down_zero, 0)

    def up_zero(n, _):
        half = lax.rem(n, 2)
        slot = 2 + half
        slope_in(n, half).wait()

        @pl.when(n < TILES - 1)
        def _():
            slope_in(n + 1, 1 - half).start()

        @pl.when(n >= 2)
        def _():
            emit_copy(0, n - 2, slot).wait()

        for rc in range(BLOCKS):
            rows = slice(BLOCK * rc, BLOCK * rc + BLOCK)
            tile[rows] = (gp[4 * half + rc] * dot_t(g[rows], wd[0, tile_cols(n), :])).astype(BF16)
        emit(0, n, slot, dot(ut0[...], tile[...]))
        return 0

    lax.fori_loop(0, TILES, up_zero, 0)
    for n in (TILES - 2, TILES - 1):
        emit_copy(1, n, n % 2).wait()
        emit_copy(0, n, 2 + n % 2).wait()


def local_grads(x_rows, dh_rows, w_up, w_down, proj_up, proj_down):
    hbm = pl.BlockSpec(memory_space=pl.ANY)
    dma = pltpu.SemaphoreType.DMA
    return pl.pallas_call(
        grad_kernel,
        out_shape=(jax.ShapeDtypeStruct((4, 4, 4, 4, 2, 2, 8, 256), F32),
                   jax.ShapeDtypeStruct((TILES, BLOCKS, BLOCK, TILE), F32)),
        in_specs=[hbm] * 6,
        out_specs=(hbm, hbm),
        scratch_shapes=[
            pltpu.VMEM((2048, 768), BF16),
            pltpu.VMEM((2048, 768), BF16),
            pltpu.VMEM((2, 768, 2048), BF16),
            pltpu.VMEM((2, 2048, 768), BF16),
            pltpu.VMEM((2, 768, 256), BF16),
            pltpu.VMEM((2, 768, 256), BF16),
            pltpu.VMEM((2048, 2048), BF16),
            pltpu.VMEM((2048, 2048), BF16),
            pltpu.VMEM((256, 2048), BF16),
            pltpu.VMEM((256, 2048), BF16),
            pltpu.VMEM((256, 2048), BF16),
            pltpu.VMEM((TILES, BLOCK, TILE), F32),
            pltpu.VMEM((2048, TILE), BF16),
            pltpu.VMEM((4, 2, 4, 2, 2, 8, 256), F32),
            dma((8,)), dma((2,)), dma((4,)),
        ],
        compiler_params=pltpu.CompilerParams(vmem_limit_bytes=67_043_328),
    )(x_rows, dh_rows, w_up, w_down, proj_up, proj_down)


class Torus:
    def __init__(self):
        me = lax.axis_index("data")
        self.core = lax.rem(me, 2)
        chip = me // 2
        self.coords = (chip // 16, lax.rem(chip // 4, 4), lax.rem(chip, 4))
        self.partner = me + 1 - 2 * self.core

    def coord(self, axis, offset):
        return lax.rem(self.coords[axis] + offset, 4)

    def peer(self, axis, offset):
        z, y, x = (self.coord(a, offset) if a == axis else self.coords[a] for a in range(3))
        return ((z * 4 + y) * 4 + x) * 2 + self.core


def remote(src, dst, send_sem, recv_sem, device):
    return pltpu.make_async_remote_copy(
        src_ref=src, dst_ref=dst, send_sem=send_sem, recv_sem=recv_sem,
        device_id=(device,), device_id_type=MESH,
    )


def entry_barrier(torus):
    barrier = pltpu.get_barrier_semaphore()
    pl.semaphore_signal(barrier, inc=1, device_id=(torus.partner,), device_id_type=MESH)
    for axis in range(3):
        for offset in (1, 2, 3):
            pl.semaphore_signal(barrier, inc=1, device_id=(torus.peer(axis, offset),), device_id_type=MESH)
    pl.semaphore_wait(barrier, 10)


def at_axis(axes, axis, index):
    return tuple(index if a == axis else slice(None) for a in axes)


class Reducer:
    def __init__(self, torus, own, pair, rb1, part1, rb2, part2, rb3, red, gath, sems):
        self.torus = torus
        self.src = (own, part1, part2)
        self.got = (rb1, rb2, rb3)
        self.pair, self.red, self.gath = pair, red, gath
        self.rs_send, self.rs_recv, self.ag_send, self.ag_recv, self.swap_send, self.swap_recv = sems
        self.pending = []
        self.inbound = {}

    def add_pair(self, m):
        own, pair = self.src[0], self.pair

        def add_plane(z, _):
            own[m, z] = own[m, z] + pair[m, z]
            return 0

        lax.fori_loop(0, 4, add_plane, 0)

    def start(self, cp, key):
        cp.start()
        self.pending.append(cp)
        self.inbound.setdefault(key, []).append(cp)

    def arrive(self, key):
        for cp in self.inbound[key]:
            cp.wait_recv()

    def scatter(self, phase, m):
        for k, (half, lane, width) in enumerate(PIECES):
            order = ORDERS[COLOURS[m][k]]
            axis = order[phase]
            axes = tuple(a for a in range(3) if a not in order[:phase])
            tail = (half, slice(None), pl.ds(lane, width))
            for offset in (1, 2, 3):
                where = at_axis(axes, axis, self.torus.coord(axis, offset))
                rest = (slice(None),) * (len(axes) - 1)
                self.start(remote(
                    self.src[phase].at[(m,) + where + tail], self.got[phase].at[(m, offset - 1) + rest + tail],
                    self.rs_send.at[phase, m, k, offset - 1], self.rs_recv.at[phase, m, k, offset - 1],
                    self.torus.peer(axis, offset)), ("rs", phase, m, k))

    def collect(self, phase, m):
        for k, (half, lane, width) in enumerate(PIECES):
            order = ORDERS[COLOURS[m][k]]
            axis = order[phase]
            axes = tuple(a for a in range(3) if a not in order[:phase])
            tail = (half, slice(None), slice(lane, lane + width))
            rest = (slice(None),) * (len(axes) - 1)
            self.arrive(("rs", phase, m, k))
            got = self.got[phase]
            total = self.src[phase][(m,) + at_axis(axes, axis, self.torus.coords[axis]) + tail]
            for other in range(3):
                total = total + got[(m, other) + rest + tail]
            if phase < 2:
                self.src[phase + 1][(m,) + rest + tail] = total
            else:
                self.red[m, 8 * half:8 * half + 8, lane:lane + width] = total

    def update(self, m, moment, variance):
        z, y, x = self.torus.coords
        new_mom, new_var, direction = adam_shard(moment, variance, self.red[m])
        self.gath[m, z, y, x, self.torus.core] = direction
        return new_mom, new_var

    def spread(self, phase, m):
        for j in range(2):
            order = ORDERS[UNITS[m][j]][::-1]
            axis = order[phase]
            where = tuple(slice(None) if a in order[:phase] else self.torus.coords[a] for a in range(3))
            ref = self.gath.at[(m,) + where + (self.torus.core, slice(None), pl.ds(128 * j, 128))]
            for offset in (1, 2, 3):
                self.start(remote(
                    ref, ref, self.ag_send.at[phase, m, j, offset - 1], self.ag_recv.at[phase, m, j, offset - 1],
                    self.torus.peer(axis, offset)), ("ag", phase, m))

    def spread_arrive(self, phase, m):
        self.arrive(("ag", phase, m))

    def swap(self, m):
        ref = self.gath.at[m, :, :, :, self.torus.core]
        self.start(remote(ref, ref, self.swap_send.at[m], self.swap_recv.at[m], self.torus.partner), ("swap", m))

    def finish(self):
        for cp in self.pending:
            cp.wait_send()


def update_kernel(r_hbm, mom_up, var_up, mom_down, var_down, dir_out, mom_up_out, var_up_out, mom_down_out,
                  var_down_out, own, pair, rb1, part1, rb2, part2, rb3, red, gath, load_sem, pair_send, pair_recv,
                  rs_send, rs_recv, ag_send, ag_recv, swap_send, swap_recv, out_sem):
    torus = Torus()
    net = Reducer(torus, own, pair, rb1, part1, rb2, part2, rb3, red, gath,
                  (rs_send, rs_recv, ag_send, ag_recv, swap_send, swap_recv))
    order = (3, 2, 1, 0)
    loads = {}
    for m in order:
        loads[m] = pltpu.make_async_copy(r_hbm.at[m, :, :, :, torus.core], own.at[m], load_sem.at[m])
        loads[m].start()
    entry_barrier(torus)
    for m in order:
        net.start(remote(r_hbm.at[m, :, :, :, 1 - torus.core], pair.at[m], pair_send.at[m], pair_recv.at[m],
                         torus.partner), ("pair", m))
    for m in order:
        loads[m].wait()
        net.arrive(("pair", m))
        net.add_pair(m)
        net.scatter(0, m)
    for phase in (0, 1):
        for m in order:
            net.collect(phase, m)
            net.scatter(phase + 1, m)
    state = ((mom_up, var_up, mom_up_out, var_up_out), (mom_down, var_down, mom_down_out, var_down_out))
    for m in order:
        net.collect(2, m)
        mom, var, mom_out, var_out = state[m % 2]
        mom_out[m // 2], var_out[m // 2] = net.update(m, mom[m // 2], var[m // 2])
        net.spread(0, m)
    for phase in (0, 1):
        for m in order:
            net.spread_arrive(phase, m)
            net.spread(phase + 1, m)
    for m in order:
        net.spread_arrive(2, m)
        net.swap(m)
    outs = []
    for m in order:
        net.arrive(("swap", m))
        cp = pltpu.make_async_copy(gath.at[m], dir_out.at[m], out_sem.at[m])
        cp.start()
        outs.append(cp)
    net.finish()
    for cp in outs:
        cp.wait()


def reduce_update(parts, moments):
    dma = pltpu.SemaphoreType.DMA
    hbm = pl.BlockSpec(memory_space=pl.ANY)
    vmem = pl.BlockSpec(memory_space=pltpu.VMEM)
    shard = jax.ShapeDtypeStruct((2, 16, 256), F32)
    return pl.pallas_call(
        update_kernel,
        out_shape=(jax.ShapeDtypeStruct((4, 4, 4, 4, 2, 16, 256), BF16),) + (shard,) * 4,
        in_specs=[hbm] + [vmem] * 4,
        out_specs=(hbm,) + (vmem,) * 4,
        scratch_shapes=[
            pltpu.VMEM((4, 4, 4, 4, 2, 8, 256), F32),
            pltpu.VMEM((4, 4, 4, 4, 2, 8, 256), F32),
            pltpu.VMEM((4, 3, 4, 4, 2, 8, 256), F32),
            pltpu.VMEM((4, 4, 4, 2, 8, 256), F32),
            pltpu.VMEM((4, 3, 4, 2, 8, 256), F32),
            pltpu.VMEM((4, 4, 2, 8, 256), F32),
            pltpu.VMEM((4, 3, 2, 8, 256), F32),
            pltpu.VMEM((4, 16, 256), F32),
            pltpu.VMEM((4, 4, 4, 4, 2, 16, 256), BF16),
            dma((4,)), dma((4,)), dma((4,)),
            dma((3, 4, 3, 3)), dma((3, 4, 3, 3)),
            dma((3, 4, 2, 3)), dma((3, 4, 2, 3)),
            dma((4,)), dma((4,)), dma((4,)),
        ],
        compiler_params=pltpu.CompilerParams(collective_id=0, has_side_effects=True),
    )(parts, *moments)


def weight_kernel(dir_up, dir_down, w_up, w_down, proj_up, proj_down, new_up, new_down):
    new_up[0] = (w_up[0] - SCALE * dot_t(proj_up[0], dir_up[0])).astype(BF16)
    new_down[0] = (w_down[0] - SCALE * dot_t(dir_down[0], proj_down[0])).astype(BF16)


def new_weights(directions, w_up, w_down, proj_up, proj_down):
    width = 512
    up_spec = pl.BlockSpec((1, 768, width), lambda l, n: (l, 0, n))
    down_spec = pl.BlockSpec((1, width, 768), lambda l, n: (l, n, 0))
    proj_spec = pl.BlockSpec((1, 768, 256), lambda l, n: (l, 0, 0))
    return pl.pallas_call(
        weight_kernel,
        grid=(2, 2048 // width),
        out_shape=(jax.ShapeDtypeStruct(w_up.shape, BF16), jax.ShapeDtypeStruct(w_down.shape, BF16)),
        in_specs=[
            pl.BlockSpec((1, width, 256), lambda l, n: (2 * l, n, 0)),
            pl.BlockSpec((1, width, 256), lambda l, n: (2 * l + 1, n, 0)),
            up_spec, down_spec, proj_spec, proj_spec,
        ],
        out_specs=(up_spec, down_spec),
    )(directions, directions, w_up, w_down, proj_up, proj_down)


def solution(mesh):
    def local_step(x_loc, dh_loc, w_up, w_down, proj_up, proj_down, mom_up, var_up, mom_down, var_down):
        parts, _ = local_grads(x_loc, dh_loc, w_up, w_down, proj_up, proj_down)
        moments = (jnp.swapaxes(mom_up, 1, 2), jnp.swapaxes(var_up, 1, 2), mom_down, var_down)
        directions, *moments = reduce_update(parts, moments)
        weights = new_weights(directions.reshape(4, 2048, 256), w_up, w_down, proj_up, proj_down)
        return (*weights, jnp.swapaxes(moments[0], 1, 2), jnp.swapaxes(moments[1], 1, 2), moments[2], moments[3])

    tok_spec = P('data', None)
    up_spec = P(None, None, 'data')
    down_spec = P(None, 'data', None)
    return jax.shard_map(
        local_step,
        mesh=mesh,
        in_specs=(tok_spec, tok_spec, P(), P(), P(), P(), up_spec, up_spec, down_spec, down_spec),
        out_specs=(P(), P(), up_spec, up_spec, down_spec, down_spec),
        check_vma=False,
    )
```

time: 1110 us -> 157 us (0.14)
  waiting for transfers between devices: 889 us -> 0 us
  matrix products: 161 us -> 0 us
  Pallas kernels: 0 us -> 153 us
  local copies, waits for them, and re-layouts: 27.2 us -> 2.48 us
  between operations: 14.5 us -> 0.69 us
  other arithmetic: 12 us -> 0 us
    reduce_scatter x1 -> x0, waiting for transfers between devices: 642 us -> none  [local_step(): lax.psum_scatter(part_down, 'data', scatter_dimension=1, tiled=True)]
    dot_general x22 -> x0, matrix products: 161 us -> none  [the longest x8 70.4 us: contract_rows(): lax.dot_general(lhs, rhs, (((0,), (0,)), ((), ())), preferred_element_typ...]
    pallas_call x0 -> x3, Pallas kernels: none -> 153 us  [the longest x1 79.3 us: local_grads(): pl.pallas_call(grad_kernel, out_shape=(jax.ShapeDtypeStruct((4, 4, 4, 4,...]
    all_gather x2 -> x0, waiting for transfers between devices: 130 us -> none  [the longest x1 70 us: local_step(): new_w_up = lax.all_gather(new_up_loc, 'data', axis=2, tiled=True)]
    unnamed x5 -> x0, waiting for transfers between devices: 117 us -> none
    unnamed x56 -> x12, local copies, waits for them, and re-layouts: 18.8 us -> 2.48 us
    add x4 -> x0, other arithmetic: 12 us -> none  [the longest x1 5.78 us: local_step(): red_up = scattered[0][0] + scattered[1][0]]
  transfers between devices with their start and end apart: 4 -> 0, of which waited for: 4 -> 0; matrix products, arithmetic and copies ran while one was open for 5% -> 0% of each run, Pallas kernels for 0% -> 0%
where the time goes in v1:
time: 157 us; the launch traced here: 156 us
  Pallas kernels  153 us (97%)
  local copies, waits for them, and re-layouts  2.48 us (2%)
    pallas_call x1, Pallas kernels, local_grads(): pl.pallas_call(grad_kernel, out_shape=(jax.ShapeDtypeStruct((4, 4, 4, 4,...  79.3 us
    pallas_call x1, Pallas kernels, reduce_update(): pl.pallas_call(update_kernel, out_shape=(jax.ShapeDtypeStruct((4, 4, 4, 4...  59.8 us
    pallas_call x1, Pallas kernels, new_weights(): pl.pallas_call(weight_kernel, grid=(2, 2048 // width), out_shape=(jax.Sha...  13.8 us

profile of v1, /device:TPU:1, one launch (start us, length us, event | category | flops | bytes accessed | tf_op | source)
XLA Modules:
  0.0 156.1 jit_solution(9625231547898401424)
XLA Ops:
  0.6 79.3 %shard_map.145 = (f32[4,4,4,4,2,2,8,256]{7,6,5,4,3,2,1,0:T(8,128)}, f32[8,4,512,256]{3,2,1,0:T(8,128)}) custom-call(bf16[2048,768]{1,0:T(8,128)(2,1)} %x_hbm.1, bf16[2048,768]{1,0:T(8,128)(2,1)} %dh_hbm.1, bf16[2,768,2048]{2,1,0:T(8,128)(2,1)} %w_up.1, bf16[2,2048,768]{2,1,0:T(8,128)(2,1)} %w_down.1, bf16[2,768,256]{2,1,0:T(8,128)(2,1)} %proj_up.1, ...), custom_call_target="tpu_custom_call" | custom-call | tf_op jit(solution)/shard_map/pallas_call | solution.py:199
  79.9 59.8 %shard_map.146 = (bf16[4,4,4,4,2,16,256]{6,5,4,3,2,1,0:T(8,128)(2,1)}, f32[2,16,256]{2,1,0:T(8,128)}, f32[2,16,256]{2,1,0:T(8,128)}, f32[2,16,256]{2,1,0:T(8,128)}, f32[2,16,256]{2,1,0:T(8,128)}) custom-call(f32[4,4,4,4,2,2,8,256]{7,6,5,4,3,2,1,0:T(8,128)} %get-tuple-element.14.r_hbm, f32[2,16,256]{2,1,0:T(8,128)} %bitcast.7, f32[2,16,256]{2,1,0:T(8,128)} %bitcast.8, ...), custom_call_target="tpu_custom_call" | custom-call | tf_op jit(solution)/shard_map/pallas_call | solution.py:403
  139.7 0.0 copy-start.3
  139.7 0.0 copy-start.2
  139.7 0.0 copy-start.1
  139.7 0.0 copy-start
  139.7 13.8 %shard_map.147 = (bf16[2,768,2048]{2,1,0:T(8,128)(2,1)}, bf16[2,2048,768]{2,1,0:T(8,128)(2,1)}) custom-call(bf16[4,2048,256]{2,1,0:T(8,128)(2,1)} %bitcast.5, bf16[4,2048,256]{2,1,0:T(8,128)(2,1)} %bitcast.6, bf16[2,768,2048]{2,1,0:T(8,128)(2,1)} %w_up.1, bf16[2,2048,768]{2,1,0:T(8,128)(2,1)} %w_down.1, bf16[2,768,256]{2,1,0:T(8,128)(2,1)} %proj_up.1, ...), custom_call_target="tpu_custom_call" | custom-call | tf_op jit(solution)/shard_map/pallas_call | solution.py:437
  153.6 0.0 copy-done.3
  153.6 0.6 copy.20
  154.2 0.0 copy-done.2
  154.2 0.6 copy.21
  154.8 0.0 copy-done.1
  154.8 0.6 copy.22
  155.5 0.0 copy-done
  155.5 0.6 copy.23
Async XLA Ops:
  139.7 13.9 %copy-start.3 = (f32[2,16,256]{2,1,0:T(8,128)S(1)}, f32[2,16,256]{2,1,0:T(8,128)}, u32[]{:S(2)}) copy-start(f32[2,16,256]{2,1,0:T(8,128)} %get-tuple-element.18) | copy-start | bytes 98308
  139.7 14.5 %copy-start.2 = (f32[2,16,256]{2,1,0:T(8,128)S(1)}, f32[2,16,256]{2,1,0:T(8,128)}, u32[]{:S(2)}) copy-start(f32[2,16,256]{2,1,0:T(8,128)} %get-tuple-element.19) | copy-start | bytes 98308
  139.7 15.1 %copy-start.1 = (f32[2,16,256]{2,1,0:T(8,128)S(1)}, f32[2,16,256]{2,1,0:T(8,128)}, u32[]{:S(2)}) copy-start(f32[2,16,256]{2,1,0:T(8,128)} %get-tuple-element.32) | copy-start | bytes 98308
  139.7 15.7 %copy-start = (f32[2,16,256]{2,1,0:T(8,128)S(1)}, f32[2,16,256]{2,1,0:T(8,128)}, u32[]{:S(2)}) copy-start(f32[2,16,256]{2,1,0:T(8,128)} %get-tuple-element.33) | copy-start | bytes 98308

commit v2 on v1

v2 whole, which is shorter than its diff:
```python
import jax
import jax.numpy as jnp
from jax import lax
from jax.experimental import pallas as pl
from jax.experimental.pallas import tpu as pltpu
from jax.sharding import PartitionSpec as P

BETA_ONE = 0.9
BETA_TWO = 0.999
EPSILON = 1e-8
STEP = 4
LEARN_RATE = 0.02
ALPHA_SCALE = 0.25
SCALE = LEARN_RATE * ALPHA_SCALE
GELU_A = 0.7978845608028654
GELU_B = 0.044715
MESH = pl.DeviceIdType.MESH
F32, BF16 = jnp.float32, jnp.bfloat16

BLOCK = 512
TILE = 256
BLOCKS = 4
TILES = 8

ORDERS = ((2, 1, 0), (1, 0, 2), (0, 2, 1))
COLOURS = ((0, 1, 2), (1, 2, 0), (2, 0, 1), (0, 1, 2))
PIECES = ((0, 0, 256), (1, 0, 128), (1, 128, 128))
UNITS = ((0, 1), (2, 0), (1, 2), (0, 1))


def dot(lhs, rhs):
    return jnp.dot(lhs, rhs, preferred_element_type=F32)


def dot_t(lhs, rhs):
    return lax.dot_general(lhs, rhs, (((1,), (1,)), ((), ())), preferred_element_type=F32)


def gelu_pair(z):
    sq = z * z
    cdf = 0.5 + 0.5 * jnp.tanh(z * (GELU_A + (GELU_A * GELU_B) * sq))
    act = z * cdf
    slope = cdf + act * ((1.0 - cdf) * (2.0 * GELU_A + (6.0 * GELU_A * GELU_B) * sq))
    return act, slope


def adam_shard(moment, variance, grad_red):
    new_mom = BETA_ONE * moment + (1.0 - BETA_ONE) * grad_red
    new_var = BETA_TWO * variance + (1.0 - BETA_TWO) * grad_red * grad_red
    bias_one = 1.0 - BETA_ONE ** STEP
    bias_two = 1.0 - BETA_TWO ** STEP
    direction = (new_mom / bias_one) / (jnp.sqrt(new_var / bias_two) + EPSILON)
    return new_mom, new_var, direction.astype(BF16)


def block_rows(i):
    return pl.ds(pl.multiple_of(i * BLOCK, BLOCK), BLOCK)


def tile_cols(n):
    return pl.ds(pl.multiple_of(n * TILE, TILE), TILE)


class Torus:
    def __init__(self):
        me = lax.axis_index("data")
        self.core = lax.rem(me, 2)
        chip = me // 2
        self.coords = (chip // 16, lax.rem(chip // 4, 4), lax.rem(chip, 4))
        self.partner = me + 1 - 2 * self.core

    def coord(self, axis, offset):
        return lax.rem(self.coords[axis] + offset, 4)

    def peer(self, axis, offset):
        z, y, x = (self.coord(a, offset) if a == axis else self.coords[a] for a in range(3))
        return ((z * 4 + y) * 4 + x) * 2 + self.core


def remote(src, dst, send_sem, recv_sem, device):
    return pltpu.make_async_remote_copy(
        src_ref=src, dst_ref=dst, send_sem=send_sem, recv_sem=recv_sem,
        device_id=(device,), device_id_type=MESH,
    )


def entry_barrier(torus):
    barrier = pltpu.get_barrier_semaphore()
    pl.semaphore_signal(barrier, inc=1, device_id=(torus.partner,), device_id_type=MESH)
    for axis in range(3):
        for offset in (1, 2, 3):
            pl.semaphore_signal(barrier, inc=1, device_id=(torus.peer(axis, offset),), device_id_type=MESH)
    return lambda: pl.semaphore_wait(barrier, 10)


def at_axis(axes, axis, index):
    return tuple(index if a == axis else slice(None) for a in axes)


class Reducer:
    def __init__(self, torus, tiles, own, pair, rb1, part1, rb2, part2, rb3, red, gath, sems):
        self.torus = torus
        self.tiles = tiles
        self.src = (own, part1, part2)
        self.got = (rb1, rb2, rb3)
        self.pair, self.red, self.gath = pair, red, gath
        (self.pair_send, self.pair_recv, self.rs_send, self.rs_recv, self.ag_send, self.ag_recv, self.swap_send,
         self.swap_recv) = sems
        self.pending = []
        self.inbound = {}

    def pair_copy(self, m, n, slot):
        where = (m, n // 2, pl.ds(2 * lax.rem(n, 2), 2))
        return remote(self.tiles.at[slot, :, :, 1 - self.torus.core], self.pair.at[where],
                      self.pair_send.at[slot], self.pair_recv.at[m, n], self.torus.partner)

    def emit(self, m, n, slot, part):
        self.tiles[slot] = part.T.reshape(2, 4, 2, 2, 8, 256)
        self.src[0][m, n // 2, pl.ds(2 * lax.rem(n, 2), 2)] = self.tiles[slot, :, :, self.torus.core]
        self.pair_copy(m, n, slot).start()

    def begin(self, m):
        for n in range(TILES):
            self.pair_copy(m, n, 0).wait_recv()
        self.add_pair(m)
        self.scatter(0, m)

    def step(self, phase, m):
        self.collect(phase, m)
        self.scatter(phase + 1, m)

    def pass_on(self, phase, m):
        self.spread_arrive(phase, m)
        self.spread(phase + 1, m)

    def add_pair(self, m):
        own, pair = self.src[0], self.pair

        def add_plane(z, _):
            own[m, z] = own[m, z] + pair[m, z]
            return 0

        lax.fori_loop(0, 4, add_plane, 0)

    def start(self, cp, key):
        cp.start()
        self.pending.append(cp)
        self.inbound.setdefault(key, []).append(cp)

    def arrive(self, key):
        for cp in self.inbound[key]:
            cp.wait_recv()

    def scatter(self, phase, m):
        for k, (half, lane, width) in enumerate(PIECES):
            order = ORDERS[COLOURS[m][k]]
            axis = order[phase]
            axes = tuple(a for a in range(3) if a not in order[:phase])
            tail = (half, slice(None), pl.ds(lane, width))
            for offset in (1, 2, 3):
                where = at_axis(axes, axis, self.torus.coord(axis, offset))
                rest = (slice(None),) * (len(axes) - 1)
                self.start(remote(
                    self.src[phase].at[(m,) + where + tail], self.got[phase].at[(m, offset - 1) + rest + tail],
                    self.rs_send.at[phase, m, k, offset - 1], self.rs_recv.at[phase, m, k, offset - 1],
                    self.torus.peer(axis, offset)), ("rs", phase, m, k))

    def collect(self, phase, m):
        for k, (half, lane, width) in enumerate(PIECES):
            order = ORDERS[COLOURS[m][k]]
            axis = order[phase]
            axes = tuple(a for a in range(3) if a not in order[:phase])
            tail = (half, slice(None), slice(lane, lane + width))
            rest = (slice(None),) * (len(axes) - 1)
            self.arrive(("rs", phase, m, k))
            got = self.got[phase]
            total = self.src[phase][(m,) + at_axis(axes, axis, self.torus.coords[axis]) + tail]
            for other in range(3):
                total = total + got[(m, other) + rest + tail]
            if phase < 2:
                self.src[phase + 1][(m,) + rest + tail] = total
            else:
                self.red[m, 8 * half:8 * half + 8, lane:lane + width] = total

    def update(self, m, moment, variance):
        z, y, x = self.torus.coords
        new_mom, new_var, direction = adam_shard(moment, variance, self.red[m])
        self.gath[m, z, y, x, self.torus.core] = direction
        return new_mom, new_var

    def spread(self, phase, m):
        for j in range(2):
            order = ORDERS[UNITS[m][j]][::-1]
            axis = order[phase]
            where = tuple(slice(None) if a in order[:phase] else self.torus.coords[a] for a in range(3))
            ref = self.gath.at[(m,) + where + (self.torus.core, slice(None), pl.ds(128 * j, 128))]
            for offset in (1, 2, 3):
                self.start(remote(
                    ref, ref, self.ag_send.at[phase, m, j, offset - 1], self.ag_recv.at[phase, m, j, offset - 1],
                    self.torus.peer(axis, offset)), ("ag", phase, m))

    def spread_arrive(self, phase, m):
        self.arrive(("ag", phase, m))

    def swap(self, m):
        self.spread_arrive(2, m)
        ref = self.gath.at[m, :, :, :, self.torus.core]
        self.start(remote(ref, ref, self.swap_send.at[m], self.swap_recv.at[m], self.torus.partner), ("swap", m))

    def finish(self):
        for cp in self.pending:
            cp.wait_send()


def step_kernel(x_hbm, dh_hbm, wu_hbm, wd_hbm, pu_hbm, pd_hbm, mom_up, var_up, mom_down, var_down,
                dir_out, mom_up_out, var_up_out, mom_down_out, var_down_out, gp_hbm,
                h, g, wu, wd, pu, pd, act, dz, ut0, gp, tile, tiles,
                own, pair, rb1, part1, rb2, part2, rb3, red, gath,
                in_sem, gp_sem, out_sem, pair_send, pair_recv, rs_send, rs_recv, ag_send, ag_recv,
                swap_send, swap_recv):
    torus = Torus()
    net = Reducer(torus, tiles, own, pair, rb1, part1, rb2, part2, rb3, red, gath,
                  (pair_send, pair_recv, rs_send, rs_recv, ag_send, ag_recv, swap_send, swap_recv))
    state = ((mom_up, var_up, mom_up_out, var_up_out), (mom_down, var_down, mom_down_out, var_down_out))

    def update(m):
        net.collect(2, m)
        mom, var, mom_out, var_out = state[m % 2]
        mom_out[m // 2], var_out[m // 2] = net.update(m, mom[m // 2], var[m // 2])
        net.spread(0, m)

    ut1, vt = wu.at[0, 0:256], wu.at[0, 256:512]
    loads = {}

    def load(name, src, dst):
        cp = pltpu.make_async_copy(src, dst, in_sem.at[len(loads)])
        cp.start()
        loads[name] = cp

    load("x", x_hbm, h)
    load("wu0", wu_hbm.at[0], wu.at[0])
    load("pu", pu_hbm, pu)
    load("wd0", wd_hbm.at[0], wd.at[0])
    load("dh", dh_hbm, g)
    load("pd", pd_hbm, pd)
    load("wu1", wu_hbm.at[1], wu.at[1])
    load("wd1", wd_hbm.at[1], wd.at[1])
    peers_ready = entry_barrier(torus)

    def slope_out(rb):
        return pltpu.make_async_copy(own, gp_hbm.at[rb], gp_sem.at[0])

    def slope_in(n, rc):
        return pltpu.make_async_copy(
            gp_hbm.at[rc, n // 2, pl.ds(2 * lax.rem(n, 2), 2)], gp.at[rc], gp_sem.at[rc])

    for name in ("x", "wu0", "pu", "wd0"):
        loads[name].wait()

    def forward_zero(rb, _):
        rows = block_rows(rb)
        ut0[:, rows] = dot(h[rows], pu[0]).astype(BF16).T
        for n in range(TILES):
            cols = slice(TILE * n, TILE * n + TILE)
            value, slope = gelu_pair(dot(h[rows], wu[0, :, cols]))
            act[rows, cols] = value.astype(BF16)
            own[n // 2, 2 * (n % 2):2 * (n % 2) + 2] = slope.reshape(2, 4, 4, 2, 8, 256)
        cp = slope_out(rb)
        cp.start()
        for k in range(3):
            cols = slice(256 * k, 256 * k + 256)
            h[rows, cols] = (h[rows, cols] + dot(act[rows], wd[0, :, cols])).astype(BF16)
        cp.wait()
        return 0

    lax.fori_loop(0, BLOCKS, forward_zero, 0)
    for name in ("dh", "pd", "wu1", "wd1"):
        loads[name].wait()
    peers_ready()

    def project_one(rb, _):
        rows = block_rows(rb)
        ut1[:, rows] = dot(h[rows], pu[1]).astype(BF16).T
        vt[:, rows] = dot(g[rows], pd[1]).astype(BF16).T
        return 0

    lax.fori_loop(0, BLOCKS, project_one, 0)

    def layer_one(n, _):
        cols = tile_cols(n)
        slot = 2 * lax.rem(n, 2)

        @pl.when(n >= 2)
        def _():
            net.pair_copy(3, n - 2, slot).wait_send()
            net.pair_copy(2, n - 2, slot + 1).wait_send()

        for rc in range(BLOCKS):
            rows = slice(BLOCK * rc, BLOCK * rc + BLOCK)
            value, slope = gelu_pair(dot(h[rows], wu[1, :, cols]))
            tile[rows] = value.astype(BF16)
            dz[rows, cols] = (slope * dot_t(g[rows], wd[1, cols, :])).astype(BF16)
        net.emit(3, n, slot, dot(vt[...], tile[...]))
        net.emit(2, n, slot + 1, dot(ut1[...], dz[:, cols]))
        return 0

    lax.fori_loop(0, TILES, layer_one, 0)

    def input_grad(rb, _):
        rows = block_rows(rb)
        for k in range(3):
            cols = slice(256 * k, 256 * k + 256)
            g[rows, cols] = (g[rows, cols] + dot_t(dz[rows], wu[1, cols, :])).astype(BF16)
        vt[:, rows] = dot(g[rows], pd[0]).astype(BF16).T
        return 0

    lax.fori_loop(0, 1, input_grad, 0)
    net.begin(3)
    net.begin(2)
    lax.fori_loop(1, BLOCKS, input_grad, 0)
    for n in (TILES - 2, TILES - 1):
        net.pair_copy(3, n, 2 * (n % 2)).wait_send()
        net.pair_copy(2, n, 2 * (n % 2) + 1).wait_send()

    def down_zero(n, _):
        slot = lax.rem(n, 2)

        @pl.when(n >= 2)
        def _():
            net.pair_copy(1, n - 2, slot).wait_send()

        net.emit(1, n, slot, dot(vt[...], act[:, tile_cols(n)]))
        return 0

    for rc in range(BLOCKS):
        slope_in(0, rc).start()
    lax.fori_loop(0, TILES, down_zero, 0)

    def up_zero(n, _):
        slot = 2 + lax.rem(n, 2)
        after = lax.min(n + 1, TILES - 1)

        @pl.when(n >= 2)
        def _():
            net.pair_copy(0, n - 2, slot).wait_send()

        for rc in range(BLOCKS):
            rows = slice(BLOCK * rc, BLOCK * rc + BLOCK)
            slope_in(n, rc).wait()
            d_act = dot_t(g[rows], wd[0, tile_cols(n), :])
            tile[rows] = (gp[rc].reshape(BLOCK, TILE) * d_act).astype(BF16)
            if rc:
                slope_in(after, rc - 1).start()
        slope_in(after, BLOCKS - 1).start()
        net.emit(0, n, slot, dot(ut0[...], tile[...]))
        return 0

    lax.fori_loop(0, 1, up_zero, 0)
    net.begin(1)
    lax.fori_loop(1, 3, up_zero, 0)
    net.step(0, 3)
    net.step(0, 2)
    lax.fori_loop(3, 5, up_zero, 0)
    net.step(1, 3)
    net.step(1, 2)
    lax.fori_loop(5, 7, up_zero, 0)
    update(3)
    update(2)
    net.step(0, 1)
    lax.fori_loop(7, 8, up_zero, 0)
    for rc in range(BLOCKS):
        slope_in(TILES - 1, rc).wait()
    net.begin(0)
    net.pass_on(0, 3)
    net.pass_on(0, 2)
    net.step(1, 1)
    net.step(0, 0)
    net.pass_on(1, 3)
    net.pass_on(1, 2)
    update(1)
    net.step(1, 0)
    net.pass_on(0, 1)
    update(0)
    net.swap(3)
    net.swap(2)
    net.pass_on(1, 1)
    net.pass_on(0, 0)
    outs = []

    def result(m):
        net.arrive(("swap", m))
        cp = pltpu.make_async_copy(gath.at[m], dir_out.at[m], out_sem.at[m])
        cp.start()
        outs.append(cp)

    result(3)
    result(2)
    net.pass_on(1, 0)
    net.swap(1)
    net.swap(0)
    result(1)
    result(0)
    for n in (TILES - 2, TILES - 1):
        net.pair_copy(1, n, n % 2).wait_send()
        net.pair_copy(0, n, 2 + n % 2).wait_send()
    net.finish()
    for cp in outs:
        cp.wait()


def train_step(x_rows, dh_rows, w_up, w_down, proj_up, proj_down, moments):
    hbm = pl.BlockSpec(memory_space=pl.ANY)
    vmem = pl.BlockSpec(memory_space=pltpu.VMEM)
    dma = pltpu.SemaphoreType.DMA
    shard = jax.ShapeDtypeStruct((2, 16, 256), F32)
    return pl.pallas_call(
        step_kernel,
        out_shape=(jax.ShapeDtypeStruct((4, 4, 4, 4, 2, 16, 256), BF16),) + (shard,) * 4
        + (jax.ShapeDtypeStruct((BLOCKS, 4, 4, 4, 4, 2, 8, 256), F32),),
        in_specs=[hbm] * 6 + [vmem] * 4,
        out_specs=(hbm,) + (vmem,) * 4 + (hbm,),
        scratch_shapes=[
            pltpu.VMEM((2048, 768), BF16),
            pltpu.VMEM((2048, 768), BF16),
            pltpu.VMEM((2, 768, 2048), BF16),
            pltpu.VMEM((2, 2048, 768), BF16),
            pltpu.VMEM((2, 768, 256), BF16),
            pltpu.VMEM((2, 768, 256), BF16),
            pltpu.VMEM((2048, 2048), BF16),
            pltpu.VMEM((2048, 2048), BF16),
            pltpu.VMEM((256, 2048), BF16),
            pltpu.VMEM((BLOCKS, 2, 4, 4, 2, 8, 256), F32),
            pltpu.VMEM((2048, TILE), BF16),
            pltpu.VMEM((4, 2, 4, 2, 2, 8, 256), F32),
            pltpu.VMEM((4, 4, 4, 4, 2, 8, 256), F32),
            pltpu.VMEM((4, 4, 4, 4, 2, 8, 256), F32),
            pltpu.VMEM((4, 3, 4, 4, 2, 8, 256), F32),
            pltpu.VMEM((4, 4, 4, 2, 8, 256), F32),
            pltpu.VMEM((4, 3, 4, 2, 8, 256), F32),
            pltpu.VMEM((4, 4, 2, 8, 256), F32),
            pltpu.VMEM((4, 3, 2, 8, 256), F32),
            pltpu.VMEM((4, 16, 256), F32),
            pltpu.VMEM((4, 4, 4, 4, 2, 16, 256), BF16),
            dma((8,)), dma((BLOCKS,)), dma((4,)), dma((4,)), dma((4, TILES)),
            dma((3, 4, 3, 3)), dma((3, 4, 3, 3)),
            dma((3, 4, 2, 3)), dma((3, 4, 2, 3)),
            dma((4,)), dma((4,)),
        ],
        compiler_params=pltpu.CompilerParams(
            collective_id=0, has_side_effects=True, vmem_limit_bytes=67_043_328),
    )(x_rows, dh_rows, w_up, w_down, proj_up, proj_down, *moments)


def weight_kernel(dir_up, dir_down, w_up, w_down, proj_up, proj_down, *refs):
    moments, new_up, new_down, outs = refs[:4], refs[4], refs[5], refs[6:]

    @pl.when((pl.program_id(0) == 0) & (pl.program_id(1) == 0))
    def _():
        for src, dst in zip(moments, outs):
            dst[...] = src[...]

    new_up[0] = (w_up[0] - SCALE * dot_t(proj_up[0], dir_up[0])).astype(BF16)
    new_down[0] = (w_down[0] - SCALE * dot_t(dir_down[0], proj_down[0])).astype(BF16)


def new_weights(directions, w_up, w_down, proj_up, proj_down, moments):
    width = 512
    up_spec = pl.BlockSpec((1, 768, width), lambda l, n: (l, 0, n))
    down_spec = pl.BlockSpec((1, width, 768), lambda l, n: (l, n, 0))
    proj_spec = pl.BlockSpec((1, 768, 256), lambda l, n: (l, 0, 0))
    shard_spec = pl.BlockSpec((2, 16, 256), lambda l, n: (0, 0, 0))
    return pl.pallas_call(
        weight_kernel,
        grid=(2, 2048 // width),
        out_shape=(jax.ShapeDtypeStruct(w_up.shape, BF16), jax.ShapeDtypeStruct(w_down.shape, BF16))
        + (jax.ShapeDtypeStruct((2, 16, 256), F32),) * 4,
        in_specs=[
            pl.BlockSpec((1, width, 256), lambda l, n: (2 * l, n, 0)),
            pl.BlockSpec((1, width, 256), lambda l, n: (2 * l + 1, n, 0)),
            up_spec, down_spec, proj_spec, proj_spec,
        ] + [shard_spec] * 4,
        out_specs=(up_spec, down_spec) + (shard_spec,) * 4,
    )(directions, directions, w_up, w_down, proj_up, proj_down, *moments)


def solution(mesh):
    def local_step(x_loc, dh_loc, w_up, w_down, proj_up, proj_down, mom_up, var_up, mom_down, var_down):
        moments = (jnp.swapaxes(mom_up, 1, 2), jnp.swapaxes(var_up, 1, 2), mom_down, var_down)
        directions, *moments, _ = train_step(x_loc, dh_loc, w_up, w_down, proj_up, proj_down, moments)
        new_up, new_down, *moments = new_weights(
            directions.reshape(4, 2048, 256), w_up, w_down, proj_up, proj_down, moments)
        return (new_up, new_down, jnp.swapaxes(moments[0], 1, 2), jnp.swapaxes(moments[1], 1, 2), moments[2], moments[3])

    tok_spec = P('data', None)
    up_spec = P(None, None, 'data')
    down_spec = P(None, 'data', None)
    return jax.shard_map(
        local_step,
        mesh=mesh,
        in_specs=(tok_spec, tok_spec, P(), P(), P(), P(), up_spec, up_spec, down_spec, down_spec),
        out_specs=(P(), P(), up_spec, up_spec, down_spec, down_spec),
        check_vma=False,
    )
```

time: 157 us -> 160 us (1.019)
  Pallas kernels: 153 us -> 159 us
  local copies, waits for them, and re-layouts: 2.48 us -> 0 us
    pallas_call x2 -> x1, Pallas kernels: 139 us -> 145 us  [train_step(): pl.pallas_call(step_kernel, out_shape=(jax.ShapeDtypeStruct((4, 4, 4, 4,...]
    unnamed x12 -> x0, local copies, waits for them, and re-layouts: 2.48 us -> none
where the time goes in v2:
time: 160 us
  Pallas kernels  159 us (99%)
    pallas_call x1, Pallas kernels, train_step(): pl.pallas_call(step_kernel, out_shape=(jax.ShapeDtypeStruct((4, 4, 4, 4,...  145 us
    pallas_call x1, Pallas kernels, new_weights(): pl.pallas_call(weight_kernel, grid=(2, 2048 // width), out_shape=(jax.Sha...  14.2 us

profile of v2, /device:TPU:1, one launch (start us, length us, event | category | flops | bytes accessed | tf_op | source)
XLA Modules:
  0.0 159.7 jit_solution(17746730217164054945)
XLA Ops:
  0.6 144.7 %shard_map.145 = (bf16[4,4,4,4,2,16,256]{6,5,4,3,2,1,0:T(8,128)(2,1)}, f32[2,16,256]{2,1,0:T(8,128)}, f32[2,16,256]{2,1,0:T(8,128)}, f32[2,16,256]{2,1,0:T(8,128...) custom-call(bf16[2048,768]{1,0:T(8,128)(2,1)} %x_hbm.1, bf16[2048,768]{1,0:T(8,128)(2,1)} %dh_hbm.1, ...), custom_call_target="tpu_custom_call" | custom-call | tf_op jit(solution)/shard_map/pallas_call | solution.py:416
  145.3 14.2 %shard_map.146 = (bf16[2,768,2048]{2,1,0:T(8,128)(2,1)}, bf16[2,2048,768]{2,1,0:T(8,128)(2,1)}, f32[2,16,256]{2,1,0:T(8,128)}, f32[2,16,256]{2,1,0:T(8,128)}, f3...) custom-call(bf16[4,2048,256]{2,1,0:T(8,128)(2,1)} %bitcast.5, bf16[4,2048,256]{2,1,0:T(8,128)(2,1)} %bitcast.6, ...), custom_call_target="tpu_custom_call" | custom-call | tf_op jit(solution)/shard_map/pallas_call | solution.py:472

commit v3 on v2

--- a/solution.py
+++ b/solution.py
@@ -15,8 +15,12 @@
 GELU_A = 0.7978845608028654
 GELU_B = 0.044715
 MESH = pl.DeviceIdType.MESH
+ALL = slice(None)
+ROWS, WIDTH, FF, RANK = 2048, 768, 2048, 256
 F32, BF16 = jnp.float32, jnp.bfloat16
 
+PIECE = (2, 4, 4, 2, 8, RANK)
+DIRECTIONS = (4,) * 4 + (2, 16, RANK)
 BLOCK = 512
 TILE = 256
 BLOCKS = 4
@@ -26,6 +30,17 @@
 COLOURS = ((0, 1, 2), (1, 2, 0), (2, 0, 1), (0, 1, 2))
 PIECES = ((0, 0, 256), (1, 0, 128), (1, 128, 128))
 UNITS = ((0, 1), (2, 0), (1, 2), (0, 1))
+SCHEDULE = (
+    (2, "all1 line3 line2"),
+    (4, "plane3 plane2"),
+    (6, "adam3 adam2 line1"),
+    (8, "pass3 pass2 plane1"),
+)
+LAST = ("begin0",)
+TAIL = (
+    "fan3 fan2 adam1 line0", "plane0 pass1", "adam0 swap3 swap2",
+    "fan1 pass0 out3 out2", "fan0 swap1 swap0",
+)
 
 
 def dot(lhs, rhs):
@@ -94,7 +109,7 @@
 
 
 def at_axis(axes, axis, index):
-    return tuple(index if a == axis else slice(None) for a in axes)
+    return tuple(index if a == axis else ALL for a in axes)
 
 
 class Reducer:
@@ -119,11 +134,38 @@
         self.src[0][m, n // 2, pl.ds(2 * lax.rem(n, 2), 2)] = self.tiles[slot, :, :, self.torus.core]
         self.pair_copy(m, n, slot).start()
 
+    def slab(self, m, z):
+        own, pair = self.src[0], self.pair
+        for half in range(2):
+            self.pair_copy(m, 2 * z + half, 0).wait_recv()
+        own[m, z] = own[m, z] + pair[m, z]
+        for k, (half, lane, width) in enumerate(PIECES):
+            axis = ORDERS[COLOURS[m][k]][0]
+            tail = (half, ALL, pl.ds(lane, width))
+            if axis == 0:
+                offset = lax.rem(z + 4 - self.torus.coords[0], 4)
+
+                @pl.when(offset > 0)
+                def _():
+                    self.copy(own.at[(m, z) + (ALL,) * 2 + tail],
+                              self.got[0].at[(m, offset - 1) + (ALL,) * 2 + tail],
+                              (0, m, k, offset - 1), self.torus.peer(0, offset)).start()
+                continue
+            for offset in (1, 2, 3):
+                where = at_axis((1, 2), axis, self.torus.coord(axis, offset))
+                self.copy(own.at[(m, z) + where + tail], self.got[0].at[(m, offset - 1, z, ALL) + tail],
+                          (0, m, k, offset - 1), self.torus.peer(axis, offset)).start()
+
     def begin(self, m):
-        for n in range(TILES):
-            self.pair_copy(m, n, 0).wait_recv()
-        self.add_pair(m)
-        self.scatter(0, m)
+        self.slab(m, 3)
+        self.scatter(0, m, False)
+
+    def begin_all(self, m):
+        lax.fori_loop(0, 3, lambda z, _: (self.slab(m, z), 0)[1], 0)
+        self.begin(m)
+
+    def copy(self, src, dst, sem, device):
+        return remote(src, dst, self.rs_send.at[sem], self.rs_recv.at[sem], device)
 
     def step(self, phase, m):
         self.collect(phase, m)
@@ -133,17 +175,9 @@
         self.spread_arrive(phase, m)
         self.spread(phase + 1, m)
 
-    def add_pair(self, m):
-        own, pair = self.src[0], self.pair
-
-        def add_plane(z, _):
-            own[m, z] = own[m, z] + pair[m, z]
-            return 0
-
-        lax.fori_loop(0, 4, add_plane, 0)
-
-    def start(self, cp, key):
-        cp.start()
+    def start(self, cp, key, go=True):
+        if go:
+            cp.start()
         self.pending.append(cp)
         self.inbound.setdefault(key, []).append(cp)
 
@@ -151,27 +185,26 @@
         for cp in self.inbound[key]:
             cp.wait_recv()
 
-    def scatter(self, phase, m):
+    def scatter(self, phase, m, go=True):
         for k, (half, lane, width) in enumerate(PIECES):
             order = ORDERS[COLOURS[m][k]]
             axis = order[phase]
             axes = tuple(a for a in range(3) if a not in order[:phase])
-            tail = (half, slice(None), pl.ds(lane, width))
+            tail = (half, ALL, pl.ds(lane, width))
             for offset in (1, 2, 3):
                 where = at_axis(axes, axis, self.torus.coord(axis, offset))
-                rest = (slice(None),) * (len(axes) - 1)
-                self.start(remote(
+                rest = (ALL,) * (len(axes) - 1)
+                self.start(self.copy(
                     self.src[phase].at[(m,) + where + tail], self.got[phase].at[(m, offset - 1) + rest + tail],
-                    self.rs_send.at[phase, m, k, offset - 1], self.rs_recv.at[phase, m, k, offset - 1],
-                    self.torus.peer(axis, offset)), ("rs", phase, m, k))
+                    (phase, m, k, offset - 1), self.torus.peer(axis, offset)), ("rs", phase, m, k), go)
 
     def collect(self, phase, m):
         for k, (half, lane, width) in enumerate(PIECES):
             order = ORDERS[COLOURS[m][k]]
             axis = order[phase]
             axes = tuple(a for a in range(3) if a not in order[:phase])
-            tail = (half, slice(None), slice(lane, lane + width))
-            rest = (slice(None),) * (len(axes) - 1)
+            tail = (half, ALL, slice(lane, lane + width))
+            rest = (ALL,) * (len(axes) - 1)
             self.arrive(("rs", phase, m, k))
             got = self.got[phase]
             total = self.src[phase][(m,) + at_axis(axes, axis, self.torus.coords[axis]) + tail]
@@ -192,8 +225,8 @@
         for j in range(2):
             order = ORDERS[UNITS[m][j]][::-1]
             axis = order[phase]
-            where = tuple(slice(None) if a in order[:phase] else self.torus.coords[a] for a in range(3))
-            ref = self.gath.at[(m,) + where + (self.torus.core, slice(None), pl.ds(128 * j, 128))]
+            where = tuple(ALL if a in order[:phase] else self.torus.coords[a] for a in range(3))
+            ref = self.gath.at[(m,) + where + (self.torus.core, ALL, pl.ds(128 * j, 128))]
             for offset in (1, 2, 3):
                 self.start(remote(
                     ref, ref, self.ag_send.at[phase, m, j, offset - 1], self.ag_recv.at[phase, m, j, offset - 1],
@@ -210,6 +243,7 @@
     def finish(self):
         for cp in self.pending:
             cp.wait_send()
+        self.pending = []
 
 
 def step_kernel(x_hbm, dh_hbm, wu_hbm, wd_hbm, pu_hbm, pd_hbm, mom_up, var_up, mom_down, var_down,
@@ -223,11 +257,33 @@
                   (pair_send, pair_recv, rs_send, rs_recv, ag_send, ag_recv, swap_send, swap_recv))
     state = ((mom_up, var_up, mom_up_out, var_up_out), (mom_down, var_down, mom_down_out, var_down_out))
 
+    outs = []
+
+    def result(m):
+        net.arrive(("swap", m))
+        cp = pltpu.make_async_copy(gath.at[m], dir_out.at[m], out_sem.at[m])
+        cp.start()
+        outs.append(cp)
+
     def update(m):
         net.collect(2, m)
         mom, var, mom_out, var_out = state[m % 2]
         mom_out[m // 2], var_out[m // 2] = net.update(m, mom[m // 2], var[m // 2])
         net.spread(0, m)
+
+    moves = {
+        "begin": net.begin, "all": net.begin_all, "line": lambda m: net.step(0, m), "plane": lambda m: net.step(1, m), "adam": update,
+        "pass": lambda m: net.pass_on(0, m), "fan": lambda m: net.pass_on(1, m), "swap": net.swap, "out": result,
+    }
+
+    def play(names):
+        for name in names.split():
+            with jax.named_scope(name):
+                moves[name[:-1]](int(name[-1]))
+
+    def run(name, body, start, stop):
+        with jax.named_scope(name):
+            lax.fori_loop(start, stop, body, 0)
 
     ut1, vt = wu.at[0, 0:256], wu.at[0, 256:512]
     loads = {}
@@ -245,38 +301,48 @@
     load("pd", pd_hbm, pd)
     load("wu1", wu_hbm.at[1], wu.at[1])
     load("wd1", wd_hbm.at[1], wd.at[1])
-    peers_ready = entry_barrier(torus)
-
-    def slope_out(rb):
-        return pltpu.make_async_copy(own, gp_hbm.at[rb], gp_sem.at[0])
-
-    def slope_in(n, rc):
-        return pltpu.make_async_copy(
-            gp_hbm.at[rc, n // 2, pl.ds(2 * lax.rem(n, 2), 2)], gp.at[rc], gp_sem.at[rc])
-
-    for name in ("x", "wu0", "pu", "wd0"):
+
+    def slope_out(rb, half):
+        part = pl.ds(2 * half, 2)
+        return pltpu.make_async_copy(own.at[part], gp_hbm.at[rb, part], gp_sem.at[half])
+
+    def slope_in(n, half):
+        return pltpu.make_async_copy(gp_hbm.at[:, n // 2, pl.ds(2 * lax.rem(n, 2), 2)], gp.at[half], gp_sem.at[half])
+
+    for name in ("x", "wu0", "pu"):
         loads[name].wait()
 
     def forward_zero(rb, _):
         rows = block_rows(rb)
-        ut0[:, rows] = dot(h[rows], pu[0]).astype(BF16).T
-        for n in range(TILES):
-            cols = slice(TILE * n, TILE * n + TILE)
-            value, slope = gelu_pair(dot(h[rows], wu[0, :, cols]))
-            act[rows, cols] = value.astype(BF16)
-            own[n // 2, 2 * (n % 2):2 * (n % 2) + 2] = slope.reshape(2, 4, 4, 2, 8, 256)
-        cp = slope_out(rb)
-        cp.start()
+        for half in range(2):
+            @pl.when(rb > 0)
+            def _():
+                slope_out(rb - 1, half).wait()
+
+            for n in range(4 * half, 4 * half + 4):
+                cols = slice(TILE * n, TILE * n + TILE)
+                value, slope = gelu_pair(dot(h[rows], wu[0, :, cols]))
+                act[rows, cols] = value.astype(BF16)
+                own[n // 2, 2 * (n % 2):2 * (n % 2) + 2] = slope.reshape(PIECE)
+            if half == 0:
+                ut0[:, rows] = dot(h[rows], pu[0]).astype(BF16).T
+            slope_out(rb, half).start()
+
+        @pl.when(rb == 0)
+        def _():
+            loads["wd0"].wait()
+
         for k in range(3):
             cols = slice(256 * k, 256 * k + 256)
             h[rows, cols] = (h[rows, cols] + dot(act[rows], wd[0, :, cols])).astype(BF16)
-        cp.wait()
         return 0
 
-    lax.fori_loop(0, BLOCKS, forward_zero, 0)
+    run("fwd0", forward_zero, 0, BLOCKS)
     for name in ("dh", "pd", "wu1", "wd1"):
         loads[name].wait()
-    peers_ready()
+    peers_ready = entry_barrier(torus)
+    for half in range(2):
+        slope_out(BLOCKS - 1, half).wait()
 
     def project_one(rb, _):
         rows = block_rows(rb)
@@ -284,7 +350,7 @@
         vt[:, rows] = dot(g[rows], pd[1]).astype(BF16).T
         return 0
 
-    lax.fori_loop(0, BLOCKS, project_one, 0)
+    run("proj1", project_one, 0, BLOCKS)
 
     def layer_one(n, _):
         cols = tile_cols(n)
@@ -294,6 +360,11 @@
         def _():
             net.pair_copy(3, n - 2, slot).wait_send()
             net.pair_copy(2, n - 2, slot + 1).wait_send()
+
+        @pl.when((n >= 3) & (lax.rem(n, 2) == 1))
+        def _():
+            net.slab(3, n // 2 - 1)
+            net.slab(2, n // 2 - 1)
 
         for rc in range(BLOCKS):
             rows = slice(BLOCK * rc, BLOCK * rc + BLOCK)
@@ -304,7 +375,8 @@
         net.emit(2, n, slot + 1, dot(ut1[...], dz[:, cols]))
         return 0
 
-    lax.fori_loop(0, TILES, layer_one, 0)
+    peers_ready()
+    run("layer1", layer_one, 0, TILES)
 
     def input_grad(rb, _):
         rows = block_rows(rb)
@@ -314,96 +386,74 @@
         vt[:, rows] = dot(g[rows], pd[0]).astype(BF16).T
         return 0
 
-    lax.fori_loop(0, 1, input_grad, 0)
-    net.begin(3)
-    net.begin(2)
-    lax.fori_loop(1, BLOCKS, input_grad, 0)
+    run("g1a", input_grad, 0, 1)
+    play("begin3 begin2")
+    run("g1b", input_grad, 1, BLOCKS)
     for n in (TILES - 2, TILES - 1):
         net.pair_copy(3, n, 2 * (n % 2)).wait_send()
         net.pair_copy(2, n, 2 * (n % 2) + 1).wait_send()
 
     def down_zero(n, _):
-        slot = lax.rem(n, 2)
-
-        @pl.when(n >= 2)
-        def _():
-            net.pair_copy(1, n - 2, slot).wait_send()
+        slot = lax.rem(n, 4)
+
+        @pl.when(n >= 4)
+        def _():
+            net.pair_copy(1, n - 4, slot).wait_send()
 
         net.emit(1, n, slot, dot(vt[...], act[:, tile_cols(n)]))
         return 0
 
-    for rc in range(BLOCKS):
-        slope_in(0, rc).start()
-    lax.fori_loop(0, TILES, down_zero, 0)
-
-    def up_zero(n, _):
-        slot = 2 + lax.rem(n, 2)
-        after = lax.min(n + 1, TILES - 1)
-
-        @pl.when(n >= 2)
-        def _():
-            net.pair_copy(0, n - 2, slot).wait_send()
+    slope_in(0, 0).start()
+    run("down0", down_zero, 0, TILES)
+    for n in range(4, TILES):
+        net.pair_copy(1, n, n % 4).wait_send()
+
+    def up_rows(n):
+        half = lax.rem(n, 2)
+        slope_in(n, half).wait()
+
+        @pl.when(n < TILES - 1)
+        def _():
+            slope_in(n + 1, 1 - half).start()
 
         for rc in range(BLOCKS):
             rows = slice(BLOCK * rc, BLOCK * rc + BLOCK)
-            slope_in(n, rc).wait()
             d_act = dot_t(g[rows], wd[0, tile_cols(n), :])
-            tile[rows] = (gp[rc].reshape(BLOCK, TILE) * d_act).astype(BF16)
-            if rc:
-                slope_in(after, rc - 1).start()
-        slope_in(after, BLOCKS - 1).start()
-        net.emit(0, n, slot, dot(ut0[...], tile[...]))
+            h[rows, tile_cols(half)] = (gp[half, rc].reshape(BLOCK, TILE) * d_act).astype(BF16)
+
+    def up_sum(n):
+        net.emit(0, n, lax.rem(n, 4), dot(ut0[...], h[:, tile_cols(lax.rem(n, 2))]))
+
+    def up_zero(n, _):
+        @pl.when(n >= 5)
+        def _():
+            net.pair_copy(0, n - 5, lax.rem(n - 1, 4)).wait_send()
+
+        @pl.when((n >= 4) & (lax.rem(n, 2) == 0))
+        def _():
+            net.slab(0, n // 2 - 2)
+
+        up_rows(n)
+        up_sum(n - 1)
         return 0
 
-    lax.fori_loop(0, 1, up_zero, 0)
-    net.begin(1)
-    lax.fori_loop(1, 3, up_zero, 0)
-    net.step(0, 3)
-    net.step(0, 2)
-    lax.fori_loop(3, 5, up_zero, 0)
-    net.step(1, 3)
-    net.step(1, 2)
-    lax.fori_loop(5, 7, up_zero, 0)
-    update(3)
-    update(2)
-    net.step(0, 1)
-    lax.fori_loop(7, 8, up_zero, 0)
-    for rc in range(BLOCKS):
-        slope_in(TILES - 1, rc).wait()
-    net.begin(0)
-    net.pass_on(0, 3)
-    net.pass_on(0, 2)
-    net.step(1, 1)
-    net.step(0, 0)
-    net.pass_on(1, 3)
-    net.pass_on(1, 2)
-    update(1)
-    net.step(1, 0)
-    net.pass_on(0, 1)
-    update(0)
-    net.swap(3)
-    net.swap(2)
-    net.pass_on(1, 1)
-    net.pass_on(0, 0)
-    outs = []
-
-    def result(m):
-        net.arrive(("swap", m))
-        cp = pltpu.make_async_copy(gath.at[m], dir_out.at[m], out_sem.at[m])
-        cp.start()
-        outs.append(cp)
-
-    result(3)
-    result(2)
-    net.pass_on(1, 0)
-    net.swap(1)
-    net.swap(0)
-    result(1)
-    result(0)
-    for n in (TILES - 2, TILES - 1):
-        net.pair_copy(1, n, n % 2).wait_send()
-        net.pair_copy(0, n, 2 + n % 2).wait_send()
+    up_rows(0)
+    first = 1
+    for last, names in SCHEDULE:
+        run(f"up{first}", up_zero, first, last)
+        play(names)
+        first = last
+    net.pair_copy(0, 3, 3).wait_send()
+    up_sum(TILES - 1)
+    net.slab(0, 2)
+    for names in LAST:
+        play(names)
+    for names in TAIL:
+        play(names)
+    for n in range(4, TILES):
+        net.pair_copy(0, n, n % 4).wait_send()
     net.finish()
+    play("out1 out0")
     for cp in outs:
         cp.wait()
 
@@ -412,36 +462,37 @@
     hbm = pl.BlockSpec(memory_space=pl.ANY)
     vmem = pl.BlockSpec(memory_space=pltpu.VMEM)
     dma = pltpu.SemaphoreType.DMA
-    shard = jax.ShapeDtypeStruct((2, 16, 256), F32)
+    shard = jax.ShapeDtypeStruct((2, 16, RANK), F32)
+
+    def sums(lines, *lead):
+        return pltpu.VMEM(lead + (4,) * lines + (2, 8, RANK), F32)
+
     return pl.pallas_call(
         step_kernel,
-        out_shape=(jax.ShapeDtypeStruct((4, 4, 4, 4, 2, 16, 256), BF16),) + (shard,) * 4
-        + (jax.ShapeDtypeStruct((BLOCKS, 4, 4, 4, 4, 2, 8, 256), F32),),
+        out_shape=(jax.ShapeDtypeStruct(DIRECTIONS, BF16),) + (shard,) * 4
+        + (jax.ShapeDtypeStruct((BLOCKS, 4) + (4,) * 3 + (2, 8, RANK), F32),),
         in_specs=[hbm] * 6 + [vmem] * 4,
         out_specs=(hbm,) + (vmem,) * 4 + (hbm,),
         scratch_shapes=[
-            pltpu.VMEM((2048, 768), BF16),
-            pltpu.VMEM((2048, 768), BF16),
-            pltpu.VMEM((2, 768, 2048), BF16),
-            pltpu.VMEM((2, 2048, 768), BF16),
-            pltpu.VMEM((2, 768, 256), BF16),
-            pltpu.VMEM((2, 768, 256), BF16),
-            pltpu.VMEM((2048, 2048), BF16),
-            pltpu.VMEM((2048, 2048), BF16),
-            pltpu.VMEM((256, 2048), BF16),
-            pltpu.VMEM((BLOCKS, 2, 4, 4, 2, 8, 256), F32),
-            pltpu.VMEM((2048, TILE), BF16),
-            pltpu.VMEM((4, 2, 4, 2, 2, 8, 256), F32),
-            pltpu.VMEM((4, 4, 4, 4, 2, 8, 256), F32),
-            pltpu.VMEM((4, 4, 4, 4, 2, 8, 256), F32),
-            pltpu.VMEM((4, 3, 4, 4, 2, 8, 256), F32),
-            pltpu.VMEM((4, 4, 4, 2, 8, 256), F32),
-            pltpu.VMEM((4, 3, 4, 2, 8, 256), F32),
-            pltpu.VMEM((4, 4, 2, 8, 256), F32),
-            pltpu.VMEM((4, 3, 2, 8, 256), F32),
-            pltpu.VMEM((4, 16, 256), F32),
-            pltpu.VMEM((4, 4, 4, 4, 2, 16, 256), BF16),
-            dma((8,)), dma((BLOCKS,)), dma((4,)), dma((4,)), dma((4, TILES)),
+            pltpu.VMEM((ROWS, WIDTH), BF16),
+            pltpu.VMEM((ROWS, WIDTH), BF16),
+            pltpu.VMEM(w_up.shape, BF16),
+            pltpu.VMEM(w_down.shape, BF16),
+            pltpu.VMEM(proj_up.shape, BF16),
+            pltpu.VMEM(proj_down.shape, BF16),
+            pltpu.VMEM((ROWS, FF), BF16),
+            pltpu.VMEM((ROWS, FF), BF16),
+            pltpu.VMEM((RANK, ROWS), BF16),
+            pltpu.VMEM((2, BLOCKS) + PIECE, F32),
+            pltpu.VMEM((ROWS, TILE), BF16),
+            pltpu.VMEM((4, 2, 4, 2, 2, 8, RANK), F32),
+            sums(3, 4), sums(3, 4),
+            sums(2, 4, 3), sums(2, 4),
+            sums(1, 4, 3), sums(1, 4),
+            sums(0, 4, 3),
+            pltpu.VMEM((4, 16, RANK), F32),
+            pltpu.VMEM(DIRECTIONS, BF16),
+            dma((8,)), dma((2,)), dma((4,)), dma((4,)), dma((4, TILES)),
             dma((3, 4, 3, 3)), dma((3, 4, 3, 3)),
             dma((3, 4, 2, 3)), dma((3, 4, 2, 3)),
             dma((4,)), dma((4,)),

time: 160 us -> 151 us (0.944)
  Pallas kernels: 159 us -> 150 us
    pallas_call x1, Pallas kernels: 145 us -> 135 us  [train_step(): pl.pallas_call(step_kernel, out_shape=(jax.ShapeDtypeStruct(DIRECTIONS, B...]
where the time goes in v3:
time: 151 us
  Pallas kernels  150 us (99%)
    pallas_call x1, Pallas kernels, train_step(): pl.pallas_call(step_kernel, out_shape=(jax.ShapeDtypeStruct(DIRECTIONS, B...  135 us
    pallas_call x1, Pallas kernels, new_weights(): pl.pallas_call(weight_kernel, grid=(2, 2048 // width), out_shape=(jax.Sha...  14.2 us

profile of v3, /device:TPU:1, one launch (start us, length us, event | category | flops | bytes accessed | tf_op | source)
XLA Modules:
  0.0 150.5 jit_solution(16092382289412547889)
XLA Ops:
  0.6 135.5 %shard_map.145 = (bf16[4,4,4,4,2,16,256]{6,5,4,3,2,1,0:T(8,128)(2,1)}, f32[2,16,256]{2,1,0:T(8,128)}, f32[2,16,256]{2,1,0:T(8,128)}, f32[2,16,256]{2,1,0:T(8,128...) custom-call(bf16[2048,768]{1,0:T(8,128)(2,1)} %x_hbm.1, bf16[2048,768]{1,0:T(8,128)(2,1)} %dh_hbm.1, ...), custom_call_target="tpu_custom_call" | custom-call | tf_op jit(solution)/shard_map/pallas_call | solution.py:470
  136.1 14.2 %shard_map.146 = (bf16[2,768,2048]{2,1,0:T(8,128)(2,1)}, bf16[2,2048,768]{2,1,0:T(8,128)(2,1)}, f32[2,16,256]{2,1,0:T(8,128)}, f32[2,16,256]{2,1,0:T(8,128)}, f3...) custom-call(bf16[4,2048,256]{2,1,0:T(8,128)(2,1)} %bitcast.5, bf16[4,2048,256]{2,1,0:T(8,128)(2,1)} %bitcast.6, ...), custom_call_target="tpu_custom_call" | custom-call | tf_op jit(solution)/shard_map/pallas_call | solution.py:523

commit v4 on v3

--- a/solution.py
+++ b/solution.py
@@ -31,16 +31,13 @@
 PIECES = ((0, 0, 256), (1, 0, 128), (1, 128, 128))
 UNITS = ((0, 1), (2, 0), (1, 2), (0, 1))
 SCHEDULE = (
-    (2, "all1 line3 line2"),
-    (4, "plane3 plane2"),
-    (6, "adam3 adam2 line1"),
-    (8, "pass3 pass2 plane1"),
+    (2, "adam3 adam2"),
+    (4, "pass3 pass2"),
+    (6, "line1 fan3 fan2"),
+    (8, "plane1"),
 )
-LAST = ("begin0",)
-TAIL = (
-    "fan3 fan2 adam1 line0", "plane0 pass1", "adam0 swap3 swap2",
-    "fan1 pass0 out3 out2", "fan0 swap1 swap0",
-)
+LAST = ("begin0 swap3 swap2 adam1",)
+TAIL = ("line0 pass1 plane0 fan1", "adam0 pass0 out3 out2", "fan0 swap1")
 
 
 def dot(lhs, rhs):
@@ -247,15 +244,15 @@
 
 
 def step_kernel(x_hbm, dh_hbm, wu_hbm, wd_hbm, pu_hbm, pd_hbm, mom_up, var_up, mom_down, var_down,
-                dir_out, mom_up_out, var_up_out, mom_down_out, var_down_out, gp_hbm,
+                dir_out, state_out, gp_hbm,
                 h, g, wu, wd, pu, pd, act, dz, ut0, gp, tile, tiles,
-                own, pair, rb1, part1, rb2, part2, rb3, red, gath,
-                in_sem, gp_sem, out_sem, pair_send, pair_recv, rs_send, rs_recv, ag_send, ag_recv,
+                own, pair, rb1, part1, rb2, part2, rb3, red, gath, fresh,
+                in_sem, gp_sem, out_sem, state_sem, pair_send, pair_recv, rs_send, rs_recv, ag_send, ag_recv,
                 swap_send, swap_recv):
     torus = Torus()
     net = Reducer(torus, tiles, own, pair, rb1, part1, rb2, part2, rb3, red, gath,
                   (pair_send, pair_recv, rs_send, rs_recv, ag_send, ag_recv, swap_send, swap_recv))
-    state = ((mom_up, var_up, mom_up_out, var_up_out), (mom_down, var_down, mom_down_out, var_down_out))
+    state = ((mom_up, var_up), (mom_down, var_down))
 
     outs = []
 
@@ -267,9 +264,12 @@
 
     def update(m):
         net.collect(2, m)
-        mom, var, mom_out, var_out = state[m % 2]
-        mom_out[m // 2], var_out[m // 2] = net.update(m, mom[m // 2], var[m // 2])
+        mom, var = state[m % 2]
+        fresh[m, 0], fresh[m, 1] = net.update(m, mom[m // 2], var[m // 2])
         net.spread(0, m)
+        cp = pltpu.make_async_copy(fresh.at[m], state_out.at[m], state_sem.at[m])
+        cp.start()
+        outs.append(cp)
 
     moves = {
         "begin": net.begin, "all": net.begin_all, "line": lambda m: net.step(0, m), "plane": lambda m: net.step(1, m), "adam": update,
@@ -389,6 +389,7 @@
     run("g1a", input_grad, 0, 1)
     play("begin3 begin2")
     run("g1b", input_grad, 1, BLOCKS)
+    play("line3 line2")
     for n in (TILES - 2, TILES - 1):
         net.pair_copy(3, n, 2 * (n % 2)).wait_send()
         net.pair_copy(2, n, 2 * (n % 2) + 1).wait_send()
@@ -437,6 +438,7 @@
         up_sum(n - 1)
         return 0
 
+    play("plane3 plane2 all1")
     up_rows(0)
     first = 1
     for last, names in SCHEDULE:
@@ -453,7 +455,8 @@
     for n in range(4, TILES):
         net.pair_copy(0, n, n % 4).wait_send()
     net.finish()
-    play("out1 out0")
+    play("swap0 out1 out0")
+    net.finish()
     for cp in outs:
         cp.wait()
 
@@ -462,17 +465,16 @@
     hbm = pl.BlockSpec(memory_space=pl.ANY)
     vmem = pl.BlockSpec(memory_space=pltpu.VMEM)
     dma = pltpu.SemaphoreType.DMA
-    shard = jax.ShapeDtypeStruct((2, 16, RANK), F32)
 
     def sums(lines, *lead):
         return pltpu.VMEM(lead + (4,) * lines + (2, 8, RANK), F32)
 
     return pl.pallas_call(
         step_kernel,
-        out_shape=(jax.ShapeDtypeStruct(DIRECTIONS, BF16),) + (shard,) * 4
-        + (jax.ShapeDtypeStruct((BLOCKS, 4) + (4,) * 3 + (2, 8, RANK), F32),),
+        out_shape=(jax.ShapeDtypeStruct(DIRECTIONS, BF16), jax.ShapeDtypeStruct((4, 2, 16, RANK), F32),
+                   jax.ShapeDtypeStruct((BLOCKS, 4) + (4,) * 3 + (2, 8, RANK), F32)),
         in_specs=[hbm] * 6 + [vmem] * 4,
-        out_specs=(hbm,) + (vmem,) * 4 + (hbm,),
+        out_specs=(hbm,) * 3,
         scratch_shapes=[
             pltpu.VMEM((ROWS, WIDTH), BF16),
             pltpu.VMEM((ROWS, WIDTH), BF16),
@@ -492,7 +494,8 @@
             sums(0, 4, 3),
             pltpu.VMEM((4, 16, RANK), F32),
             pltpu.VMEM(DIRECTIONS, BF16),
-            dma((8,)), dma((2,)), dma((4,)), dma((4,)), dma((4, TILES)),
+            pltpu.VMEM((4, 2, 16, RANK), F32),
+            dma((8,)), dma((2,)), dma((4,)), dma((4,)), dma((4,)), dma((4, TILES)),
             dma((3, 4, 3, 3)), dma((3, 4, 3, 3)),
             dma((3, 4, 2, 3)), dma((3, 4, 2, 3)),
             dma((4,)), dma((4,)),
@@ -503,18 +506,19 @@
 
 
 def weight_kernel(dir_up, dir_down, w_up, w_down, proj_up, proj_down, *refs):
-    moments, new_up, new_down, outs = refs[:4], refs[4], refs[5], refs[6:]
+    state, new_up, new_down, outs = refs[0], refs[1], refs[2], refs[3:]
 
     @pl.when((pl.program_id(0) == 0) & (pl.program_id(1) == 0))
     def _():
-        for src, dst in zip(moments, outs):
-            dst[...] = src[...]
+        for m in range(4):
+            for k in range(2):
+                outs[2 * (m % 2) + k][m // 2] = state[m, k]
 
     new_up[0] = (w_up[0] - SCALE * dot_t(proj_up[0], dir_up[0])).astype(BF16)
     new_down[0] = (w_down[0] - SCALE * dot_t(dir_down[0], proj_down[0])).astype(BF16)
 
 
-def new_weights(directions, w_up, w_down, proj_up, proj_down, moments):
+def new_weights(directions, w_up, w_down, proj_up, proj_down, state):
     width = 512
     up_spec = pl.BlockSpec((1, 768, width), lambda l, n: (l, 0, n))
     down_spec = pl.BlockSpec((1, width, 768), lambda l, n: (l, n, 0))
@@ -529,17 +533,18 @@
             pl.BlockSpec((1, width, 256), lambda l, n: (2 * l, n, 0)),
             pl.BlockSpec((1, width, 256), lambda l, n: (2 * l + 1, n, 0)),
             up_spec, down_spec, proj_spec, proj_spec,
-        ] + [shard_spec] * 4,
+            pl.BlockSpec(state.shape, lambda l, n: (0, 0, 0, 0)),
+        ],
         out_specs=(up_spec, down_spec) + (shard_spec,) * 4,
-    )(directions, directions, w_up, w_down, proj_up, proj_down, *moments)
+    )(directions, directions, w_up, w_down, proj_up, proj_down, state)
 
 
 def solution(mesh):
     def local_step(x_loc, dh_loc, w_up, w_down, proj_up, proj_down, mom_up, var_up, mom_down, var_down):
         moments = (jnp.swapaxes(mom_up, 1, 2), jnp.swapaxes(var_up, 1, 2), mom_down, var_down)
-        directions, *moments, _ = train_step(x_loc, dh_loc, w_up, w_down, proj_up, proj_down, moments)
+        directions, state, _ = train_step(x_loc, dh_loc, w_up, w_down, proj_up, proj_down, moments)
         new_up, new_down, *moments = new_weights(
-            directions.reshape(4, 2048, 256), w_up, w_down, proj_up, proj_down, moments)
+            directions.reshape(4, 2048, 256), w_up, w_down, proj_up, proj_down, state)
         return (new_up, new_down, jnp.swapaxes(moments[0], 1, 2), jnp.swapaxes(moments[1], 1, 2), moments[2], moments[3])
 
     tok_spec = P('data', None)

time: 151 us -> 147 us (0.974)
  Pallas kernels: 150 us -> 146 us
    pallas_call x1, Pallas kernels: 135 us -> 132 us  [train_step(): pl.pallas_call(step_kernel, out_shape=(jax.ShapeDtypeStruct(DIRECTIONS, B...]
where the time goes in v4:
time: 147 us
  Pallas kernels  146 us (99%)
    pallas_call x1, Pallas kernels, train_step(): pl.pallas_call(step_kernel, out_shape=(jax.ShapeDtypeStruct(DIRECTIONS, B...  132 us
    pallas_call x1, Pallas kernels, new_weights(): pl.pallas_call(weight_kernel, grid=(2, 2048 // width), out_shape=(jax.Sha...  14.3 us

profile of v4, /device:TPU:1, one launch (start us, length us, event | category | flops | bytes accessed | tf_op | source)
XLA Modules:
  0.0 147.0 jit_solution(17234646295047789318)
XLA Ops:
  0.6 132.1 %shard_map.145 = (bf16[4,4,4,4,2,16,256]{6,5,4,3,2,1,0:T(8,128)(2,1)}, f32[4,2,16,256]{3,2,1,0:T(8,128)}, f32[4,4,4,4,4,2,8,256]{7,6,5,4,3,2,1,0:T(8,128)}) custom-call(bf16[2048,768]{1,0:T(8,128)(2,1)} %x_hbm.1, bf16[2048,768]{1,0:T(8,128)(2,1)} %dh_hbm.1, bf16[2,768,2048]{2,1,0:T(8,128)(2,1)} %w_up.1, bf16[2,2048,768]{2,1,0:T(8,128)(2,1)} %w_down.1, ...), custom_call_target="tpu_custom_call" | custom-call | tf_op jit(solution)/shard_map/pallas_call | solution.py:472
  132.7 14.3 %shard_map.146 = (bf16[2,768,2048]{2,1,0:T(8,128)(2,1)}, bf16[2,2048,768]{2,1,0:T(8,128)(2,1)}, f32[2,16,256]{2,1,0:T(8,128)}, f32[2,16,256]{2,1,0:T(8,128)}, f3...) custom-call(bf16[4,2048,256]{2,1,0:T(8,128)(2,1)} %bitcast.5, bf16[4,2048,256]{2,1,0:T(8,128)(2,1)} %bitcast.6, ...), custom_call_target="tpu_custom_call" | custom-call | tf_op jit(solution)/shard_map/pallas_call | solution.py:527

commit v5 on v4

--- a/solution.py
+++ b/solution.py
@@ -293,14 +293,17 @@
         cp.start()
         loads[name] = cp
 
-    load("x", x_hbm, h)
+    first, others = pl.ds(0, BLOCK), pl.ds(BLOCK, ROWS - BLOCK)
+    load("x", x_hbm.at[first], h.at[first])
     load("wu0", wu_hbm.at[0], wu.at[0])
     load("pu", pu_hbm, pu)
     load("wd0", wd_hbm.at[0], wd.at[0])
+    load("xs", x_hbm.at[others], h.at[others])
     load("dh", dh_hbm, g)
     load("pd", pd_hbm, pd)
     load("wu1", wu_hbm.at[1], wu.at[1])
     load("wd1", wd_hbm.at[1], wd.at[1])
+    peers_ready = entry_barrier(torus)
 
     def slope_out(rb, half):
         part = pl.ds(2 * half, 2)
@@ -309,7 +312,7 @@
     def slope_in(n, half):
         return pltpu.make_async_copy(gp_hbm.at[:, n // 2, pl.ds(2 * lax.rem(n, 2), 2)], gp.at[half], gp_sem.at[half])
 
-    for name in ("x", "wu0", "pu"):
+    for name in ("x", "wu0"):
         loads[name].wait()
 
     def forward_zero(rb, _):
@@ -324,14 +327,15 @@
                 value, slope = gelu_pair(dot(h[rows], wu[0, :, cols]))
                 act[rows, cols] = value.astype(BF16)
                 own[n // 2, 2 * (n % 2):2 * (n % 2) + 2] = slope.reshape(PIECE)
-            if half == 0:
-                ut0[:, rows] = dot(h[rows], pu[0]).astype(BF16).T
             slope_out(rb, half).start()
 
         @pl.when(rb == 0)
         def _():
             loads["wd0"].wait()
-
+            loads["xs"].wait()
+            loads["pu"].wait()
+
+        ut0[:, rows] = dot(h[rows], pu[0]).astype(BF16).T
         for k in range(3):
             cols = slice(256 * k, 256 * k + 256)
             h[rows, cols] = (h[rows, cols] + dot(act[rows], wd[0, :, cols])).astype(BF16)
@@ -340,7 +344,6 @@
     run("fwd0", forward_zero, 0, BLOCKS)
     for name in ("dh", "pd", "wu1", "wd1"):
         loads[name].wait()
-    peers_ready = entry_barrier(torus)
     for half in range(2):
         slope_out(BLOCKS - 1, half).wait()
 
@@ -495,7 +498,7 @@
             pltpu.VMEM((4, 16, RANK), F32),
             pltpu.VMEM(DIRECTIONS, BF16),
             pltpu.VMEM((4, 2, 16, RANK), F32),
-            dma((8,)), dma((2,)), dma((4,)), dma((4,)), dma((4,)), dma((4, TILES)),
+            dma((9,)), dma((2,)), dma((4,)), dma((4,)), dma((4,)), dma((4, TILES)),
             dma((3, 4, 3, 3)), dma((3, 4, 3, 3)),
             dma((3, 4, 2, 3)), dma((3, 4, 2, 3)),
             dma((4,)), dma((4,)),
@@ -505,38 +508,80 @@
     )(x_rows, dh_rows, w_up, w_down, proj_up, proj_down, *moments)
 
 
-def weight_kernel(dir_up, dir_down, w_up, w_down, proj_up, proj_down, *refs):
-    state, new_up, new_down, outs = refs[0], refs[1], refs[2], refs[3:]
-
-    @pl.when((pl.program_id(0) == 0) & (pl.program_id(1) == 0))
-    def _():
-        for m in range(4):
-            for k in range(2):
-                outs[2 * (m % 2) + k][m // 2] = state[m, k]
-
-    new_up[0] = (w_up[0] - SCALE * dot_t(proj_up[0], dir_up[0])).astype(BF16)
-    new_down[0] = (w_down[0] - SCALE * dot_t(dir_down[0], proj_down[0])).astype(BF16)
+def weight_kernel(dirs, w_up, w_down, proj_up, proj_down, state, new_up, new_down, mom_up, var_up, mom_down, var_down,
+                  n_buf, up_buf, down_buf, pu, pd, s_buf, in_sem, small_sem, out_sem, state_sem):
+    def chunk(q):
+        return q // 4, pl.ds(pl.multiple_of(BLOCK * lax.rem(q, 4), BLOCK), BLOCK)
+
+    def inputs(q):
+        l, part = chunk(q)
+        pairs = (
+            (dirs.at[2 * l, part], n_buf.at[0, l, part]), (dirs.at[2 * l + 1, part], n_buf.at[1, l, part]),
+            (w_up.at[l, ALL, part], up_buf.at[l, ALL, part]), (w_down.at[l, part], down_buf.at[l, part]),
+        )
+        return [pltpu.make_async_copy(src, dst, in_sem.at[k, q]) for k, (src, dst) in enumerate(pairs)]
+
+    def outputs(q):
+        l, part = chunk(q)
+        pairs = ((up_buf.at[l, ALL, part], new_up.at[l, ALL, part]), (down_buf.at[l, part], new_down.at[l, part]))
+        return [pltpu.make_async_copy(src, dst, out_sem.at[k, q]) for k, (src, dst) in enumerate(pairs)]
+
+    def each(copies, action):
+        def body(q, _):
+            for cp in copies(q):
+                action(cp)
+            return 0
+
+        lax.fori_loop(0, TILES, body, 0)
+
+    smalls = [pltpu.make_async_copy(src, dst, small_sem.at[k])
+              for k, (src, dst) in enumerate(((proj_up, pu), (proj_down, pd), (state, s_buf)))]
+    for cp in smalls:
+        cp.start()
+    each(inputs, lambda cp: cp.start())
+    for cp in smalls:
+        cp.wait()
+    leaving = []
+    for m in range(4):
+        for k, dst in enumerate(((mom_up, var_up), (mom_down, var_down))[m % 2]):
+            leaving.append(pltpu.make_async_copy(s_buf.at[m, k], dst.at[m // 2], state_sem.at[m, k]))
+            leaving[-1].start()
+
+    def compute(q, _):
+        l, part = chunk(q)
+        for cp in inputs(q):
+            cp.wait()
+        up_buf[l, :, part] = (up_buf[l, :, part] - SCALE * dot_t(pu[l], n_buf[0, l, part])).astype(BF16)
+        down_buf[l, part] = (down_buf[l, part] - SCALE * dot_t(n_buf[1, l, part], pd[l])).astype(BF16)
+        for cp in outputs(q):
+            cp.start()
+        return 0
+
+    lax.fori_loop(0, TILES, compute, 0)
+    each(outputs, lambda cp: cp.wait())
+    for cp in leaving:
+        cp.wait()
 
 
 def new_weights(directions, w_up, w_down, proj_up, proj_down, state):
-    width = 512
-    up_spec = pl.BlockSpec((1, 768, width), lambda l, n: (l, 0, n))
-    down_spec = pl.BlockSpec((1, width, 768), lambda l, n: (l, n, 0))
-    proj_spec = pl.BlockSpec((1, 768, 256), lambda l, n: (l, 0, 0))
-    shard_spec = pl.BlockSpec((2, 16, 256), lambda l, n: (0, 0, 0))
+    hbm = pl.BlockSpec(memory_space=pl.ANY)
+    dma = pltpu.SemaphoreType.DMA
     return pl.pallas_call(
         weight_kernel,
-        grid=(2, 2048 // width),
         out_shape=(jax.ShapeDtypeStruct(w_up.shape, BF16), jax.ShapeDtypeStruct(w_down.shape, BF16))
-        + (jax.ShapeDtypeStruct((2, 16, 256), F32),) * 4,
-        in_specs=[
-            pl.BlockSpec((1, width, 256), lambda l, n: (2 * l, n, 0)),
-            pl.BlockSpec((1, width, 256), lambda l, n: (2 * l + 1, n, 0)),
-            up_spec, down_spec, proj_spec, proj_spec,
-            pl.BlockSpec(state.shape, lambda l, n: (0, 0, 0, 0)),
+        + (jax.ShapeDtypeStruct((2, 16, RANK), F32),) * 4,
+        in_specs=[hbm] * 6,
+        out_specs=(hbm,) * 6,
+        scratch_shapes=[
+            pltpu.VMEM((2, 2, FF, RANK), BF16),
+            pltpu.VMEM(w_up.shape, BF16),
+            pltpu.VMEM(w_down.shape, BF16),
+            pltpu.VMEM(proj_up.shape, BF16),
+            pltpu.VMEM(proj_down.shape, BF16),
+            pltpu.VMEM(state.shape, F32),
+            dma((4, TILES)), dma((3,)), dma((2, TILES)), dma((4, 2)),
         ],
-        out_specs=(up_spec, down_spec) + (shard_spec,) * 4,
-    )(directions, directions, w_up, w_down, proj_up, proj_down, state)
+    )(directions, w_up, w_down, proj_up, proj_down, state)
 
 
 def solution(mesh):

time: 147 us -> 141 us (0.959)
  Pallas kernels: 146 us -> 140 us
    pallas_call x1, Pallas kernels: 132 us -> 128 us  [train_step(): pl.pallas_call(step_kernel, out_shape=(jax.ShapeDtypeStruct(DIRECTIONS, B...]
    pallas_call x1, Pallas kernels: 14.3 us -> 12 us  [new_weights(): pl.pallas_call(weight_kernel, out_shape=(jax.ShapeDtypeStruct(w_up.shape,...]
where the time goes in v5:
time: 141 us
  Pallas kernels  140 us (99%)
    pallas_call x1, Pallas kernels, train_step(): pl.pallas_call(step_kernel, out_shape=(jax.ShapeDtypeStruct(DIRECTIONS, B...  128 us
    pallas_call x1, Pallas kernels, new_weights(): pl.pallas_call(weight_kernel, out_shape=(jax.ShapeDtypeStruct(w_up.shape,...  12 us

profile of v5, /device:TPU:1, one launch (start us, length us, event | category | flops | bytes accessed | tf_op | source)
XLA Modules:
  0.0 140.5 jit_solution(7311422868191580319)
XLA Ops:
  0.6 127.7 %shard_map.145 = (bf16[4,4,4,4,2,16,256]{6,5,4,3,2,1,0:T(8,128)(2,1)}, f32[4,2,16,256]{3,2,1,0:T(8,128)}, f32[4,4,4,4,4,2,8,256]{7,6,5,4,3,2,1,0:T(8,128)}) custom-call(bf16[2048,768]{1,0:T(8,128)(2,1)} %x_hbm.1, bf16[2048,768]{1,0:T(8,128)(2,1)} %dh_hbm.1, bf16[2,768,2048]{2,1,0:T(8,128)(2,1)} %w_up.1, bf16[2,2048,768]{2,1,0:T(8,128)(2,1)} %w_down.1, ...), custom_call_target="tpu_custom_call" | custom-call | tf_op jit(solution)/shard_map/pallas_call | solution.py:475
  128.4 12.0 %shard_map.146 = (bf16[2,768,2048]{2,1,0:T(8,128)(2,1)}, bf16[2,2048,768]{2,1,0:T(8,128)(2,1)}, f32[2,16,256]{2,1,0:T(8,128)}, f32[2,16,256]{2,1,0:T(8,128)}, f3...) custom-call(bf16[4,2048,256]{2,1,0:T(8,128)(2,1)} %bitcast.5, bf16[2,768,2048]{2,1,0:T(8,128)(2,1)} %w_up.1, ...), custom_call_target="tpu_custom_call" | custom-call | tf_op jit(solution)/shard_map/pallas_call | solution.py:569

commit v6 on v5

--- a/solution.py
+++ b/solution.py
@@ -245,7 +245,7 @@
 
 def step_kernel(x_hbm, dh_hbm, wu_hbm, wd_hbm, pu_hbm, pd_hbm, mom_up, var_up, mom_down, var_down,
                 dir_out, state_out, gp_hbm,
-                h, g, wu, wd, pu, pd, act, dz, ut0, gp, tile, tiles,
+                h, g, wu, wd, pu, pd, act, dz, ut0, gp, tile, parts, tiles,
                 own, pair, rb1, part1, rb2, part2, rb3, red, gath, fresh,
                 in_sem, gp_sem, out_sem, state_sem, pair_send, pair_recv, rs_send, rs_recv, ag_send, ag_recv,
                 swap_send, swap_recv):
@@ -355,31 +355,47 @@
 
     run("proj1", project_one, 0, BLOCKS)
 
-    def layer_one(n, _):
+    def layer_rows(n):
         cols = tile_cols(n)
-        slot = 2 * lax.rem(n, 2)
-
-        @pl.when(n >= 2)
-        def _():
-            net.pair_copy(3, n - 2, slot).wait_send()
-            net.pair_copy(2, n - 2, slot + 1).wait_send()
-
-        @pl.when((n >= 3) & (lax.rem(n, 2) == 1))
-        def _():
-            net.slab(3, n // 2 - 1)
-            net.slab(2, n // 2 - 1)
-
         for rc in range(BLOCKS):
             rows = slice(BLOCK * rc, BLOCK * rc + BLOCK)
             value, slope = gelu_pair(dot(h[rows], wu[1, :, cols]))
             tile[rows] = value.astype(BF16)
             dz[rows, cols] = (slope * dot_t(g[rows], wd[1, cols, :])).astype(BF16)
-        net.emit(3, n, slot, dot(vt[...], tile[...]))
-        net.emit(2, n, slot + 1, dot(ut1[...], dz[:, cols]))
+        parts[0] = dot(vt[...], tile[...])
+        parts[1] = dot(ut1[...], dz[:, cols])
+
+    def layer_emit(n):
+        slot = 2 * lax.rem(n, 2)
+        net.emit(3, n, slot, parts[0])
+        net.emit(2, n, slot + 1, parts[1])
+
+    def layer_free(n):
+        slot = 2 * lax.rem(n, 2)
+        net.pair_copy(3, n - 2, slot).wait_send()
+        net.pair_copy(2, n - 2, slot + 1).wait_send()
+
+    def layer_one(n, _):
+        @pl.when(n >= 3)
+        def _():
+            layer_free(n - 1)
+
+        @pl.when((n >= 4) & (lax.rem(n, 2) == 0))
+        def _():
+            net.slab(3, n // 2 - 2)
+            net.slab(2, n // 2 - 2)
+
+        layer_emit(n - 1)
+        layer_rows(n)
         return 0
 
     peers_ready()
-    run("layer1", layer_one, 0, TILES)
+    layer_rows(0)
+    run("layer1", layer_one, 1, TILES)
+    layer_free(TILES - 1)
+    layer_emit(TILES - 1)
+    net.slab(3, 2)
+    net.slab(2, 2)
 
     def input_grad(rb, _):
         rows = block_rows(rb)
@@ -397,18 +413,20 @@
         net.pair_copy(3, n, 2 * (n % 2)).wait_send()
         net.pair_copy(2, n, 2 * (n % 2) + 1).wait_send()
 
-    def down_zero(n, _):
-        slot = lax.rem(n, 4)
-
-        @pl.when(n >= 4)
+    def down_zero(pair, _):
+        @pl.when(pair >= 2)
         def _():
-            net.pair_copy(1, n - 4, slot).wait_send()
-
-        net.emit(1, n, slot, dot(vt[...], act[:, tile_cols(n)]))
+            for k in range(2):
+                n = 2 * pair + k
+                net.pair_copy(1, n - 4, lax.rem(n, 4)).wait_send()
+
+        for k in range(2):
+            n = 2 * pair + k
+            net.emit(1, n, lax.rem(n, 4), dot(vt[...], act[:, tile_cols(n)]))
         return 0
 
     slope_in(0, 0).start()
-    run("down0", down_zero, 0, TILES)
+    run("down0", down_zero, 0, TILES // 2)
     for n in range(4, TILES):
         net.pair_copy(1, n, n % 4).wait_send()
 
@@ -490,6 +508,7 @@
             pltpu.VMEM((RANK, ROWS), BF16),
             pltpu.VMEM((2, BLOCKS) + PIECE, F32),
             pltpu.VMEM((ROWS, TILE), BF16),
+            pltpu.VMEM((2, RANK, TILE), F32),
             pltpu.VMEM((4, 2, 4, 2, 2, 8, RANK), F32),
             sums(3, 4), sums(3, 4),
             sums(2, 4, 3), sums(2, 4),

time: 141 us -> 141 us (level)
  no operation moved by 1% of the time
where the time goes in v6:
time: 141 us
  Pallas kernels  140 us (99%)
    pallas_call x1, Pallas kernels, train_step(): pl.pallas_call(step_kernel, out_shape=(jax.ShapeDtypeStruct(DIRECTIONS, B...  128 us
    pallas_call x1, Pallas kernels, new_weights(): pl.pallas_call(weight_kernel, out_shape=(jax.ShapeDtypeStruct(w_up.shape,...  12 us

profile of v6, /device:TPU:1, one launch (start us, length us, event | category | flops | bytes accessed | tf_op | source)
XLA Modules:
  0.0 140.8 jit_solution(9930637246823907153)
XLA Ops:
  0.6 128.0 %shard_map.145 = (bf16[4,4,4,4,2,16,256]{6,5,4,3,2,1,0:T(8,128)(2,1)}, f32[4,2,16,256]{3,2,1,0:T(8,128)}, f32[4,4,4,4,4,2,8,256]{7,6,5,4,3,2,1,0:T(8,128)}) custom-call(bf16[2048,768]{1,0:T(8,128)(2,1)} %x_hbm.1, bf16[2048,768]{1,0:T(8,128)(2,1)} %dh_hbm.1, bf16[2,768,2048]{2,1,0:T(8,128)(2,1)} %w_up.1, bf16[2,2048,768]{2,1,0:T(8,128)(2,1)} %w_down.1, ...), custom_call_target="tpu_custom_call" | custom-call | tf_op jit(solution)/shard_map/pallas_call | solution.py:493
  128.6 12.0 %shard_map.146 = (bf16[2,768,2048]{2,1,0:T(8,128)(2,1)}, bf16[2,2048,768]{2,1,0:T(8,128)(2,1)}, f32[2,16,256]{2,1,0:T(8,128)}, f32[2,16,256]{2,1,0:T(8,128)}, f3...) custom-call(bf16[4,2048,256]{2,1,0:T(8,128)(2,1)} %bitcast.5, bf16[2,768,2048]{2,1,0:T(8,128)(2,1)} %w_up.1, ...), custom_call_target="tpu_custom_call" | custom-call | tf_op jit(solution)/shard_map/pallas_call | solution.py:588
